TPU v7x, 32 devices: a 4x4x1 block of a 4x4x8 slice. The times are simulated.
32 devices in a mesh: dp: 1 (over z), tp: 4 (over y), cp: 8 (over x, core).
Axes of the slice: x: 4, y: 4, z: 1, core: 2. Of those that a mesh axis runs over, the one named last changes fastest.
The devices are a block of a 4x4x8 slice.
Arguments:
- x: bfloat16 [4096, 3072], P(('dp', 'cp'))
- doc_id: int32 [4096], P(('dp', 'cp'))
- pos_in_doc: int32 [4096], P(('dp', 'cp'))
- norm_gain: float32 [3072], replicated
- w_q: bfloat16 [3072, 3072], P(None, 'tp')
- w_k: bfloat16 [3072, 1024], P(None, 'tp')
- w_v: bfloat16 [3072, 1024], P(None, 'tp')
- w_o: bfloat16 [3072, 3072], P('tp')
- inv_freq: float32 [64], replicated
Outputs:
- output 1: bfloat16 [4096, 3072], P(('dp', 'cp'))
- output 2: bfloat16 [4096, 8, 128], P(('dp', 'cp'), 'tp')
- output 3: bfloat16 [4096, 8, 128], P(('dp', 'cp'), 'tp')
All inputs are finite; a program needn't handle non-finite values.
Results may differ from a plain program's by a relative error of at most 0.00161997.
Values are sent between devices in bfloat16 or wider.
A program may use at most 768 MiB of HBM per device.

v0:
```python
import jax
import jax.numpy as jnp
from jax import lax
from jax.sharding import PartitionSpec as P

QUERY_ROWS = 128


def rms_norm(x_in, norm_gain):
    x_f32 = x_in.astype(jnp.float32)
    inv_rms = lax.rsqrt(jnp.mean(x_f32 * x_f32, axis=-1, keepdims=True) + 1e-5)
    return (x_f32 * inv_rms * norm_gain).astype(jnp.bfloat16)


def apply_rope(vectors, cos_t, sin_t):
    half_dim = vectors.shape[-1] // 2
    lower_half = vectors[..., :half_dim].astype(jnp.float32)
    upper_half = vectors[..., half_dim:].astype(jnp.float32)
    turned = jnp.concatenate([lower_half * cos_t - upper_half * sin_t, upper_half * cos_t + lower_half * sin_t], axis=-1)
    return turned.astype(jnp.bfloat16)


def project(x_in, pos_in_doc, norm_gain, w_q, w_k, w_v, inv_freq):
    num_rows = x_in.shape[0]
    head_dim = 2 * inv_freq.shape[0]
    kv_heads = w_k.shape[1] // head_dim
    group_size = w_q.shape[1] // (head_dim * kv_heads)
    normed = rms_norm(x_in, norm_gain)
    q_new = jnp.dot(normed, w_q, preferred_element_type=jnp.float32).astype(jnp.bfloat16).reshape(num_rows, kv_heads, group_size, head_dim)
    k_new = jnp.dot(normed, w_k, preferred_element_type=jnp.float32).astype(jnp.bfloat16).reshape(num_rows, kv_heads, head_dim)
    v_new = jnp.dot(normed, w_v, preferred_element_type=jnp.float32).astype(jnp.bfloat16).reshape(num_rows, kv_heads, head_dim)
    rope_angle = pos_in_doc.astype(jnp.float32)[:, None] * inv_freq[None, :]
    cos_t = jnp.cos(rope_angle)
    sin_t = jnp.sin(rope_angle)
    q_rot = apply_rope(q_new, cos_t[:, None, None, :], sin_t[:, None, None, :])
    k_rot = apply_rope(k_new, cos_t[:, None, :], sin_t[:, None, :])
    return q_rot, k_rot, v_new


def global_index(stored_pos, local_rows, cp_size):
    piece_len = local_rows // 2
    owner = stored_pos // local_rows
    within = stored_pos % local_rows
    piece_id = jnp.where(within < piece_len, owner, 2 * cp_size - 1 - owner)
    return piece_id * piece_len + within % piece_len


def attention(q_rot, key_rows, val_rows, q_doc, q_idx, key_doc, key_idx):
    local_rows, kv_heads, group_size, head_dim = q_rot.shape
    blocks = local_rows // QUERY_ROWS
    score_scale = head_dim ** -0.5

    def attend(block_args):
        q_blk, doc_blk, idx_blk = block_args
        scores = jnp.einsum('qngd,knd->ngqk', q_blk, key_rows, preferred_element_type=jnp.float32) * score_scale
        visible = (doc_blk[:, None] == key_doc[None, :]) & (key_idx[None, :] <= idx_blk[:, None])
        scores = jnp.where(visible, scores, -1e30)
        attn_probs = jax.nn.softmax(scores, axis=-1).astype(jnp.bfloat16)
        return jnp.einsum('ngqk,knd->qngd', attn_probs, val_rows, preferred_element_type=jnp.float32).astype(jnp.bfloat16)

    attn_out = lax.map(attend, (q_rot.reshape(blocks, QUERY_ROWS, kv_heads, group_size, head_dim), q_doc.reshape(blocks, QUERY_ROWS), q_idx.reshape(blocks, QUERY_ROWS)))
    return attn_out.reshape(local_rows, kv_heads * group_size * head_dim)


def solution(mesh):
    cp_size = mesh.shape['cp']

    def local_step(x_in, doc_id, pos_in_doc, norm_gain, w_q, w_k, w_v, w_o, inv_freq):
        local_rows = x_in.shape[0]
        tokens = local_rows * cp_size
        q_rot, k_rot, v_new = project(x_in, pos_in_doc, norm_gain, w_q, w_k, w_v, inv_freq)
        k_all = lax.all_gather(k_rot, 'cp', tiled=True)
        v_all = lax.all_gather(v_new, 'cp', tiled=True)
        doc_all = lax.all_gather(doc_id, 'cp', tiled=True)
        cp_index = lax.axis_index('cp')
        q_idx = global_index(cp_index * local_rows + jnp.arange(local_rows), local_rows, cp_size)
        key_idx = global_index(jnp.arange(tokens), local_rows, cp_size)
        attn_out = attention(q_rot, k_all, v_all, doc_id, q_idx, doc_all, key_idx)
        part_sum = jnp.dot(attn_out, w_o, preferred_element_type=jnp.float32)
        full_sum = lax.psum(part_sum, 'tp')
        y_out = (x_in.astype(jnp.float32) + full_sum).astype(jnp.bfloat16)
        return y_out, k_rot, v_new

    row_spec = P(('dp', 'cp'))
    in_specs = (P(('dp', 'cp'), None), row_spec, row_spec, P(), P(None, 'tp'), P(None, 'tp'), P(None, 'tp'), P('tp', None), P())
    out_specs = (P(('dp', 'cp'), None), P(('dp', 'cp'), 'tp', None), P(('dp', 'cp'), 'tp', None))
    return jax.shard_map(local_step, mesh=mesh, in_specs=in_specs, out_specs=out_specs, check_vma=False)
```

profile of v0, /device:TPU:97, one launch (start us, length us, event | category | flops | bytes accessed | tf_op | source)
XLA Modules:
  0.0 285.2 jit_solution(6807873197066260915)
XLA Ops:
  7.2 0.0 copy-start
  7.2 0.1 all-gather.4.cloned.1.call-start
  7.3 2.7 fusion.57
  10.0 0.7 convert_element_type.50
  10.6 1.2 multiply_cosine_fusion
  11.8 0.0 copy-done
  11.8 0.0 copy-start.4
  11.9 3.1 %convolution_convert_fusion.2 = bf16[512,256]{0,1:T(8,128)(2,1)S(1)} fusion(bf16[3072,256]{1,0:T(8,128)(2,1)S(1)} %copy-done, bf16[512,3072]{1,0:T(8,128)(2,1)} %param.11, f32[3072]{0:T(1024)} %param.14, f32[512]{0:T(512)S(1)} %add_rsqrt_fusion), kind=kOutput, calls=%fused_computation.61 | convolution fusion | flops 811728896 | bytes 4995072 | tf_op jit(solution)/shard_map/dot_general | solution.py:30
  15.0 0.1 fusion.69
  15.1 0.9 copy.38
  16.0 0.1 all-gather.4.cloned.1.call-update
  16.1 0.1 all-gather.6.cloned.1.call-start
  16.1 3.6 %convolution_convert_fusion.1 = bf16[512,256]{0,1:T(8,128)(2,1)S(1)} fusion(bf16[3072,256]{1,0:T(8,128)(2,1)} %param.17, bf16[512,3072]{1,0:T(8,128)(2,1)} %param.11, f32[3072]{0:T(1024)S(1)} %copy-done.4, f32[512]{0:T(512)S(1)} %add_rsqrt_fusion), kind=kOutput, calls=%fused_computation.60 | convolution fusion | flops 811728896 | bytes 4995072 | tf_op jit(solution)/shard_map/dot_general | solution.py:31
  19.8 0.8 copy.39
  20.6 0.1 all-gather.6.cloned.1.call-update
  20.7 0.1 all-reduce.2.cloned.1.call-start
  20.8 6.0 %convolution_convert_fusion = bf16[512,768]{1,0:T(8,128)(2,1)S(1)} fusion(bf16[3072,768]{1,0:T(8,128)(2,1)} %param.15, bf16[512,3072]{1,0:T(8,128)(2,1)} %param.11, f32[3072]{0:T(1024)S(1)} %copy-done.4, f32[512]{0:T(512)S(1)} %add_rsqrt_fusion), kind=kOutput, calls=%fused_computation.59 | convolution fusion | flops 2422603776 | bytes 8665088 | tf_op jit(solution)/shard_map/dot_general | solution.py:29
  26.7 0.0 copy-start.3
  26.7 0.3 copy.37
  27.0 0.3 fusion.62
  27.3 0.1 concatenate.13
  27.4 0.1 concatenate.14
  27.5 0.5 pad_maximum_fusion
  28.0 0.6 copy.40
  28.7 19.8 %all-gather = s32[8,1,512]{2,1,0:T(1,128)S(1)} all-gather(s32[1,1,512]{2,1,0:T(1,128)S(1)} %bitcast.101), channel_id=1, replica_groups=mesh['dp'=1,'tp'=4,'cp'=8] {'cp'}, dimensions={0}, use_global_device_ids=true | all-gather | bytes 18432 | tf_op jit(solution)/shard_map/all_gather | solution.py:74
  48.5 0.0 all-gather.4.cloned.1.call-done
  48.6 3.2 %copy.41 = bf16[4096,2,128]{2,0,1:T(8,128)(2,1)} copy(bf16[4096,2,128]{2,1,0:T(2,128)(2,1)} %all-gather.4.cloned.1.call-done) | data formatting | bytes 4194304
  51.7 16.6 %all-gather.6.cloned.1.call-done = bf16[4096,2,128]{2,0,1:T(8,128)(2,1)} async-done(((bf16[512,2,128]{2,0,1:T(8,128)(2,1)}), bf16[4096,2,128]{2,0,1:T(8,128)(2,1)}) %all-gather.6.cloned.1.call-update) | async-done | bytes 2097168 | tf_op jit(solution)/shard_map/all_gather | solution.py:73
  68.4 73.7 %while.11 = (s32[]{:T(128)}, bf16[4,128,2,3,128]{4,1,3,2,0:T(8,128)(2,1)}, s32[4,128]{1,0:T(4,128)S(1)}, s32[4096]{0:T(1024)S(1)}, s32[4,128]{1,0:T(4,128)S(1)},...) while((s32[]{:T(128)}, ...), condition=%wide.region_4.5_spmd.clone, body=%wide.region_1.4_spmd.clone.sunk | while | flops 1631277056 | bytes 30860900 | solution.py:61
  68.4 0.5 compare_and_fusion.2
  68.9 10.2 %fusion.105 = (f32[2,3,128]{2,1,0:T(4,128)S(1)}, f32[2,3,128,4096]{3,2,1,0:T(8,128)}) fusion(pred[128,4096]{1,0:T(8,128)(4,1)S(1)} %compare_and_fusion.2, bf16[4096,2,128]{2,0,1:T(8,128)(2,1)} %get-tuple-element.220, bf16[4,128,2,3,128]{4,1,3,2,0:T(8,128)(2,1)S(1)} %get-tuple-element.219, s32[]{:T(128)} %get-tuple-element.205), kind=kOutput, calls=%fused_computation.102.clone.1 | convolution fusion | flops 817893376 | bytes 15404036 | tf_op jit(solution)/shard_map/while/body/eval_jaxpr/sub | solution.py:58
  79.1 7.7 %fusion.106 = bf16[4,128,2,3,128]{4,1,3,2,0:T(8,128)(2,1)} fusion(bf16[4,128,2,3,128]{4,1,3,2,0:T(8,128)(2,1)} %get-tuple-element.206, s32[]{:T(128)} %get-tuple-element.205, bf16[4096,2,128]{2,0,1:T(8,128)(2,1)} %get-tuple-element.221, f32[2,3,128,4096]{3,2,1,0:T(8,128)} %get-tuple-element.194, f32[2,3,128]{2,1,0:T(4,128)S(1)} %get-tuple-element.195), kind=kOutput, calls=%fused_computation.20.clone.1 | convolution fusion | flops 811696128 | bytes 14880256 | tf_op jit(solution)/shard_map/while/body/eval_jaxpr/ngqk,knd->qngd/dot_general | solution.py:59
  86.9 0.5 compare_and_fusion.2
  87.3 10.2 %fusion.105 = (f32[2,3,128]{2,1,0:T(4,128)S(1)}, f32[2,3,128,4096]{3,2,1,0:T(8,128)}) fusion(pred[128,4096]{1,0:T(8,128)(4,1)S(1)} %compare_and_fusion.2, bf16[4096,2,128]{2,0,1:T(8,128)(2,1)} %get-tuple-element.220, bf16[4,128,2,3,128]{4,1,3,2,0:T(8,128)(2,1)S(1)} %get-tuple-element.219, s32[]{:T(128)} %get-tuple-element.205), kind=kOutput, calls=%fused_computation.102.clone.1 | convolution fusion | flops 817893376 | bytes 15404036 | tf_op jit(solution)/shard_map/while/body/eval_jaxpr/sub | solution.py:58
  97.6 7.7 %fusion.106 = bf16[4,128,2,3,128]{4,1,3,2,0:T(8,128)(2,1)} fusion(bf16[4,128,2,3,128]{4,1,3,2,0:T(8,128)(2,1)} %get-tuple-element.206, s32[]{:T(128)} %get-tuple-element.205, bf16[4096,2,128]{2,0,1:T(8,128)(2,1)} %get-tuple-element.221, f32[2,3,128,4096]{3,2,1,0:T(8,128)} %get-tuple-element.194, f32[2,3,128]{2,1,0:T(4,128)S(1)} %get-tuple-element.195), kind=kOutput, calls=%fused_computation.20.clone.1 | convolution fusion | flops 811696128 | bytes 14880256 | tf_op jit(solution)/shard_map/while/body/eval_jaxpr/ngqk,knd->qngd/dot_general | solution.py:59
  105.3 0.5 compare_and_fusion.2
  105.8 10.2 %fusion.105 = (f32[2,3,128]{2,1,0:T(4,128)S(1)}, f32[2,3,128,4096]{3,2,1,0:T(8,128)}) fusion(pred[128,4096]{1,0:T(8,128)(4,1)S(1)} %compare_and_fusion.2, bf16[4096,2,128]{2,0,1:T(8,128)(2,1)} %get-tuple-element.220, bf16[4,128,2,3,128]{4,1,3,2,0:T(8,128)(2,1)S(1)} %get-tuple-element.219, s32[]{:T(128)} %get-tuple-element.205), kind=kOutput, calls=%fused_computation.102.clone.1 | convolution fusion | flops 817893376 | bytes 15404036 | tf_op jit(solution)/shard_map/while/body/eval_jaxpr/sub | solution.py:58
  116.0 7.7 %fusion.106 = bf16[4,128,2,3,128]{4,1,3,2,0:T(8,128)(2,1)} fusion(bf16[4,128,2,3,128]{4,1,3,2,0:T(8,128)(2,1)} %get-tuple-element.206, s32[]{:T(128)} %get-tuple-element.205, bf16[4096,2,128]{2,0,1:T(8,128)(2,1)} %get-tuple-element.221, f32[2,3,128,4096]{3,2,1,0:T(8,128)} %get-tuple-element.194, f32[2,3,128]{2,1,0:T(4,128)S(1)} %get-tuple-element.195), kind=kOutput, calls=%fused_computation.20.clone.1 | convolution fusion | flops 811696128 | bytes 14880256 | tf_op jit(solution)/shard_map/while/body/eval_jaxpr/ngqk,knd->qngd/dot_general | solution.py:59
  123.7 0.5 compare_and_fusion.2
  124.2 10.2 %fusion.105 = (f32[2,3,128]{2,1,0:T(4,128)S(1)}, f32[2,3,128,4096]{3,2,1,0:T(8,128)}) fusion(pred[128,4096]{1,0:T(8,128)(4,1)S(1)} %compare_and_fusion.2, bf16[4096,2,128]{2,0,1:T(8,128)(2,1)} %get-tuple-element.220, bf16[4,128,2,3,128]{4,1,3,2,0:T(8,128)(2,1)S(1)} %get-tuple-element.219, s32[]{:T(128)} %get-tuple-element.205), kind=kOutput, calls=%fused_computation.102.clone.1 | convolution fusion | flops 817893376 | bytes 15404036 | tf_op jit(solution)/shard_map/while/body/eval_jaxpr/sub | solution.py:58
  134.4 7.7 %fusion.106 = bf16[4,128,2,3,128]{4,1,3,2,0:T(8,128)(2,1)} fusion(bf16[4,128,2,3,128]{4,1,3,2,0:T(8,128)(2,1)} %get-tuple-element.206, s32[]{:T(128)} %get-tuple-element.205, bf16[4096,2,128]{2,0,1:T(8,128)(2,1)} %get-tuple-element.221, f32[2,3,128,4096]{3,2,1,0:T(8,128)} %get-tuple-element.194, f32[2,3,128]{2,1,0:T(4,128)S(1)} %get-tuple-element.195), kind=kOutput, calls=%fused_computation.20.clone.1 | convolution fusion | flops 811696128 | bytes 14880256 | tf_op jit(solution)/shard_map/while/body/eval_jaxpr/ngqk,knd->qngd/dot_general | solution.py:59
  142.1 1.5 copy.42
  143.6 6.9 %fusion.65 = f32[512,3072]{1,0:T(8,128)} fusion(bf16[768,3072]{1,0:T(8,128)(2,1)} %param.18, bf16[96,8,4,128]{3,2,1,0:T(4,128)(2,1)S(1)} %bitcast.96), kind=kOutput, calls=%fused_computation.70 | convolution fusion | flops 2415919104 | bytes 11796480 | tf_op jit(solution)/shard_map/dot_general | solution.py:79
  150.5 0.1 all-reduce.2.cloned.1.call-update
  150.6 0.9 copy-done.2
  151.5 0.9 copy.44
  152.3 120.0 %all-reduce.2.cloned.1.call-done = f32[512,3072]{1,0:T(8,128)} async-done(((f32[512,3072]{1,0:T(8,128)}), f32[512,3072]{1,0:T(8,128)}) %all-reduce.2.cloned.1.call-update) | async-done | bytes 6291472 | tf_op jit(solution)/shard_map/psum | solution.py:80
  272.3 6.4 %fusion.60 = bf16[512,3072]{1,0:T(8,128)(2,1)} fusion(f32[512,3072]{1,0:T(8,128)} %all-reduce.2.cloned.1.call-done, bf16[512,3072]{1,0:T(8,128)(2,1)} %param.11), kind=kLoop, calls=%fused_computation.58 | loop fusion | flops 4718592 | bytes 12582912 | tf_op jit(solution)/shard_map/convert_element_type | solution.py:81
  (17 shorter events, 0.1 us)
Async XLA Ops:
  7.2 4.7 %copy-start = (bf16[3072,256]{1,0:T(8,128)(2,1)S(1)}, bf16[3072,256]{1,0:T(8,128)(2,1)}, u32[]{:S(2)}) copy-start(bf16[3072,256]{1,0:T(8,128)(2,1)} %param.16) | copy-start | bytes 4718596
  7.2 41.4 %all-gather.4.cloned.1.call-start = ((), (), s32[]{:S(2)}) async-start(), calls=%async_computation | async-start | bytes 2359296 | tf_op jit(solution)/shard_map/all_gather | solution.py:72
  11.8 4.3 %copy-start.4 = (f32[3072]{0:T(1024)S(1)}, f32[3072]{0:T(1024)}, u32[]{:S(2)}) copy-start(f32[3072]{0:T(1024)} %param.14) | copy-start | bytes 36868
  16.1 52.3 %all-gather.6.cloned.1.call-start = ((), (), s32[]{:S(2)}) async-start(), calls=%async_computation.1 | async-start | bytes 2359296 | tf_op jit(solution)/shard_map/all_gather | solution.py:73
  19.8 1.0 copy-start.1
  20.7 251.6 %all-reduce.2.cloned.1.call-start = ((), (), s32[]{:S(2)}) async-start(), calls=%async_computation.2 | async-start | bytes 12582912 | tf_op jit(solution)/shard_map/psum | solution.py:80
  26.7 1.9 copy-start.3
  150.5 0.9 copy-start.2
Sparse Core Ops, SparseCore 0:
  16.2 26.8 all-gather.3
  45.2 23.1 all-gather.5
  150.7 121.5 all-reduce.1
where the time goes:
time: 286 us; the launch traced here: 285 us
  waiting for transfers between devices  137 us (48%)
  matrix products  91.3 us (32%)
  blocking collectives  19.8 us (7%)
  between operations  14 us (5%)
  other arithmetic  13.8 us (5%)
  local copies, waits for them, and re-layouts  9.33 us (3%)
    psum x1, waiting for transfers between devices, local_step(): full_sum = lax.psum(part_sum, 'tp')  120 us
    sub x4, matrix products, attend(): attn_probs = jax.nn.softmax(scores, axis=-1).astype(jnp.bfloat16)  40.9 us
    dot_general x4, matrix products, attend(): jnp.einsum('ngqk,knd->qngd', attn_probs, val_rows, preferred_element_type...  30.8 us
    all_gather x1, blocking collectives, local_step(): doc_all = lax.all_gather(doc_id, 'cp', tiled=True)  19.8 us
    all_gather x1, waiting for transfers between devices, local_step(): v_all = lax.all_gather(v_new, 'cp', tiled=True)  16.6 us
    dot_general x1, matrix products, local_step(): part_sum = jnp.dot(attn_out, w_o, preferred_element_type=jnp.float32)  6.87 us
    convert_element_type x1, other arithmetic, local_step(): y_out = (x_in.astype(jnp.float32) + full_sum).astype(jnp.bfloat16)  6.39 us
    dot_general x1, matrix products, project(): jnp.dot(normed, w_q, preferred_element_type=jnp.float32)  5.95 us
  transfers between devices with their start and end apart: 3, of which 2 were waited for; matrix products, arithmetic and copies ran while one was open for 6% of the time, Pallas kernels for 0%

commit v1 on v0

v1 whole, which is shorter than its diff:
```python
import functools

import jax
import jax.numpy as jnp
from jax import lax
from jax.experimental import pallas as pl
from jax.experimental.pallas import tpu as pltpu
from jax.sharding import PartitionSpec as P

MESH = pl.DeviceIdType.MESH
F32 = jnp.float32
BF16 = jnp.bfloat16
HALO = 128
BLK = 128
TILE = 256
NEG = -1e30


class Copies:
    def __init__(self, send_sems, recv_sems):
        self.send_sems, self.recv_sems, self.made = send_sems, recv_sems, {}

    def start(self, name, src, dst, device):
        slot = len(self.made)
        copy = pltpu.make_async_remote_copy(src_ref=src, dst_ref=dst, send_sem=self.send_sems.at[slot], recv_sem=self.recv_sems.at[slot], device_id=device, device_id_type=MESH)
        self.made[name] = copy
        copy.start()

    def arrived(self, name):
        self.made[name].wait_recv()

    def drain(self):
        for copy in self.made.values():
            copy.wait_send()


def layer_kernel(cp_size, tp_size, x_hbm, pos_hbm, gain_hbm, wq_hbm, wk_hbm, wv_hbm, wo_hbm, freq_hbm,
                 y_hbm, k_hbm, v_hbm, far_ref,
                 x_v, h_v, wq_v, wk_v, wv_v, w_all, transit, o_all, y_v, q_v, k_win, v_win, k_out, v_out,
                 pos_v, gain_v, freq_v, cos_v, sin_v, posb_v, pos_all, load_sems, send_sems, recv_sems):
    rows, d_model = x_v.shape
    piece = rows // 2
    half = d_model // 2
    q_cols = q_v.shape[1]
    head_dim = freq_v.shape[1] * 2
    kv_heads = k_win.shape[2] // head_dim
    group = q_cols // (kv_heads * head_dim)
    gcols = group * head_dim
    share = q_cols // cp_size
    part = share // 2

    me_c = lax.axis_index("cp")
    me_t = lax.axis_index("tp")
    up_t = {"tp": lax.rem(me_t + 1, tp_size)}
    dn_t = {"tp": lax.rem(me_t + tp_size - 1, tp_size)}
    up_x = {"cp": lax.rem(me_c + 2, cp_size)}
    dn_x = {"cp": lax.rem(me_c + cp_size - 2, cp_size)}
    mate = {"cp": me_c + 1 - 2 * lax.rem(me_c, 2)}
    nxt = {"cp": lax.rem(me_c + 1, cp_size)}
    prv = {"cp": lax.rem(me_c + cp_size - 1, cp_size)}
    mine = lax.rem(me_t, 2)
    other = 1 - mine
    my_cols = pl.multiple_of(mine * half, half)
    other_cols = pl.multiple_of(other * half, half)

    loads = {}

    def load(name, src, dst):
        copy = pltpu.make_async_copy(src, dst, load_sems.at[len(loads)])
        loads[name] = copy
        copy.start()

    load("pos", pos_hbm, pos_v)
    load("freq", freq_hbm, freq_v)
    load("gain", gain_hbm, gain_v)
    for c in range(rows // BLK):
        load(("x", c), x_hbm.at[pl.ds(c * BLK, BLK)], x_v.at[pl.ds(c * BLK, BLK)])
    load("wk", wk_hbm, wk_v)
    load("wv", wv_hbm, wv_v)
    load("wq", wq_hbm, wq_v)
    load("wo", wo_hbm.at[:, pl.ds(my_cols, half)], w_all.at[0])

    barrier = pltpu.get_barrier_semaphore()
    for d in range(1, cp_size):
        pl.semaphore_signal(barrier, inc=1, device_id={"cp": lax.rem(me_c + d, cp_size)}, device_id_type=MESH)
    for peer in (up_t, dn_t):
        pl.semaphore_signal(barrier, inc=1, device_id=peer, device_id_type=MESH)
    pl.semaphore_wait(barrier, cp_size + 1)

    rc = Copies(send_sems, recv_sems)
    row0 = pl.multiple_of(me_c * share, share)
    row1 = pl.multiple_of(me_c * share + part, part)

    def share_of(who):
        return pl.ds(pl.multiple_of(who * share, share), share)

    def part_of(who, i):
        return pl.ds(pl.multiple_of(who * share + i * part, part), part)

    rc.start("w_up", wo_hbm.at[pl.ds(row0, share), pl.ds(other_cols, half)], w_all.at[3, pl.ds(row0, share)], up_t)
    rc.start("w_dn", wo_hbm.at[pl.ds(row0, share), pl.ds(other_cols, half)], w_all.at[1, pl.ds(row0, share)], dn_t)
    rc.start("t_up", wo_hbm.at[pl.ds(row0, part), pl.ds(my_cols, half)], transit.at[0], up_t)
    rc.start("t_dn", wo_hbm.at[pl.ds(row1, part), pl.ds(my_cols, half)], transit.at[1], dn_t)
    for d in range(1, cp_size):
        rc.start(("pos", d), pos_hbm, pos_all.at[cp_size - d], {"cp": lax.rem(me_c + d, cp_size)})

    loads["pos"].wait()
    loads["freq"].wait()
    pos_all[0] = pos_v[...]
    freq = jnp.concatenate([freq_v[...], freq_v[...]], axis=1)
    sign = jnp.where(lax.broadcasted_iota(jnp.int32, (1, head_dim), 1) < head_dim // 2, -1.0, 1.0).astype(F32)
    for c in range(rows // BLK):
        pos_rows = jnp.transpose(jnp.broadcast_to(pos_v[pl.ds(c, 1), :], (BLK, BLK)))
        posb_v[pl.ds(c * BLK, BLK), :] = pos_rows
        angle = pos_rows.astype(F32) * freq
        cos_v[pl.ds(c * BLK, BLK), :] = jnp.cos(angle)
        sin_v[pl.ds(c * BLK, BLK), :] = jnp.sin(angle) * sign

    loads["gain"].wait()
    for c in range(rows // BLK):
        loads[("x", c)].wait()

        def norm(i, carry):
            at = pl.ds(pl.multiple_of(c * BLK + i * 32, 32), 32)
            x_f32 = x_v[at, :].astype(F32)
            inv_rms = lax.rsqrt(jnp.mean(x_f32 * x_f32, axis=-1, keepdims=True) + 1e-5)
            h_v[at, :] = (x_f32 * inv_rms * gain_v[...]).astype(BF16)
            return carry

        lax.fori_loop(0, BLK // 32, norm, 0)

    def rope(raw, c):
        at = pl.ds(c * BLK, BLK)
        vec = raw.astype(F32)
        return (vec * cos_v[at, :] + pltpu.roll(vec, head_dim // 2, 1) * sin_v[at, :]).astype(BF16)

    def window_at(c):
        return c * BLK // piece, pl.ds(HALO + c * BLK % piece, BLK)

    loads["wk"].wait()
    k_new = jnp.dot(h_v[...], wk_v[...], preferred_element_type=F32).astype(BF16)
    for c in range(rows // BLK):
        p, at = window_at(c)
        heads = []
        for n in range(kv_heads):
            rot = rope(k_new[c * BLK:(c + 1) * BLK, n * head_dim:(n + 1) * head_dim], c)
            k_win[p, at, n * head_dim:(n + 1) * head_dim] = rot
            heads.append(rot)
        k_out[pl.ds(c * BLK, BLK)] = jnp.stack(heads, axis=1)
    tail = pl.ds(piece, HALO)
    halo = pl.ds(0, HALO)
    rc.start("hk_a", k_win.at[0, tail], k_win.at[0, halo], nxt)
    rc.start("hk_b", k_win.at[1, tail], k_win.at[1, halo], prv)
    loads["wv"].wait()
    v_new = jnp.dot(h_v[...], wv_v[...], preferred_element_type=F32).astype(BF16)
    for c in range(rows // BLK):
        p, at = window_at(c)
        v_win[p, at, :] = v_new[c * BLK:(c + 1) * BLK]
        v_out[pl.ds(c * BLK, BLK)] = jnp.stack([v_new[c * BLK:(c + 1) * BLK, n * head_dim:(n + 1) * head_dim] for n in range(kv_heads)], axis=1)
    rc.start("hv_a", v_win.at[0, tail], v_win.at[0, halo], nxt)
    rc.start("hv_b", v_win.at[1, tail], v_win.at[1, halo], prv)
    load("k_out", k_out, k_hbm)
    load("v_out", v_out, v_hbm)

    def spread_own(r):
        at = share_of(me_c)
        rc.start(("xu", r), w_all.at[r, at], w_all.at[r, at], up_x)
        rc.start(("xd", r), w_all.at[r, at], w_all.at[r, at], dn_x)
        rc.start(("m0", r), w_all.at[r, at], w_all.at[r, at], mate)

    def spread_near(r):
        lo, hi = share_of(dn_x["cp"]), share_of(up_x["cp"])
        rc.arrived(("xu", r))
        rc.start(("fu", r), w_all.at[r, part_of(dn_x["cp"], 0)], w_all.at[r, part_of(dn_x["cp"], 0)], up_x)
        rc.start(("m1", r), w_all.at[r, lo], w_all.at[r, lo], mate)
        rc.arrived(("xd", r))
        rc.start(("fd", r), w_all.at[r, part_of(up_x["cp"], 1)], w_all.at[r, part_of(up_x["cp"], 1)], dn_x)
        rc.start(("m2", r), w_all.at[r, hi], w_all.at[r, hi], mate)

    def spread_far(r):
        far = lax.rem(me_c + cp_size // 2, cp_size)
        rc.arrived(("fu", r))
        rc.arrived(("fd", r))
        rc.start(("m3", r), w_all.at[r, share_of(far)], w_all.at[r, share_of(far)], mate)

    rc.arrived("t_up")
    rc.start("t_up2", transit.at[0], w_all.at[2, pl.ds(row0, part)], up_t)
    rc.arrived("t_dn")
    rc.start("t_dn2", transit.at[1], w_all.at[2, pl.ds(row1, part)], dn_t)
    rc.arrived("w_up")
    rc.arrived("w_dn")
    spread_own(3)
    spread_own(1)

    loads["wq"].wait()

    def project_q(i, carry):
        at = pl.ds(pl.multiple_of(i * TILE, TILE), TILE)
        q_new = jnp.dot(h_v[...], wq_v[:, at], preferred_element_type=F32).astype(BF16)
        for c in range(rows // BLK):
            for n in range(TILE // head_dim):
                rot = rope(q_new[c * BLK:(c + 1) * BLK, n * head_dim:(n + 1) * head_dim], c)
                q_v[pl.ds(c * BLK, BLK), pl.ds(pl.multiple_of(i * TILE + n * head_dim, head_dim), head_dim)] = rot
        return carry

    lax.fori_loop(0, q_cols // TILE, project_q, 0)

    rc.arrived("t_up2")
    rc.arrived("t_dn2")
    spread_own(2)

    for name in ("hk_a", "hk_b", "hv_a", "hv_b"):
        rc.arrived(name)

    @pl.when(me_c == cp_size - 1)
    def _():
        k_win[1, 0:HALO, :] = k_win[0, piece:piece + HALO, :]
        v_win[1, 0:HALO, :] = v_win[0, piece:piece + HALO, :]

    score_scale = head_dim ** -0.5
    for p in range(2):
        for n in range(kv_heads):
            cols = slice(n * head_dim, (n + 1) * head_dim)
            for b in range(piece // BLK):
                keys = HALO + (b + 1) * BLK
                at = pl.ds(p * piece + b * BLK, BLK)
                q_blk = jnp.concatenate([q_v[at, (n * group + g) * head_dim:(n * group + g + 1) * head_dim] for g in range(group)], axis=0)
                scores = lax.dot_general(q_blk, k_win[p, 0:keys, cols], (((1,), (1,)), ((), ())), preferred_element_type=F32) * score_scale
                key = lax.broadcasted_iota(jnp.int32, (BLK, keys), 1) - HALO
                row = lax.broadcasted_iota(jnp.int32, (BLK, keys), 0) + b * BLK
                back = jnp.concatenate([posb_v[at, :]] * (keys // BLK), axis=1)
                visible = (key <= row) & (key >= row - back)
                scores = jnp.where(visible[None], scores.reshape(group, BLK, keys), NEG)
                top = jnp.max(scores, axis=-1, keepdims=True)
                weights = jnp.exp(scores - top)
                probs = (weights / jnp.sum(weights, axis=-1, keepdims=True)).astype(BF16).reshape(group * BLK, keys)
                o_blk = jnp.dot(probs, v_win[p, 0:keys, cols], preferred_element_type=F32).astype(BF16)
                for g in range(group):
                    o_all[0, at, (n * group + g) * head_dim:(n * group + g + 1) * head_dim] = o_blk[g * BLK:(g + 1) * BLK]
            block = (pl.ds(p * piece, piece), pl.ds(n * gcols, gcols))
            rc.start(("ou", p, n), o_all.at[(0,) + block], o_all.at[(3,) + block], up_t)
            rc.start(("od", p, n), o_all.at[(0,) + block], o_all.at[(1,) + block], dn_t)

    def forward_o(p):
        first = (pl.ds(p * piece, piece), pl.ds(0, gcols))
        last = (pl.ds(p * piece, piece), pl.ds((kv_heads - 1) * gcols, gcols))
        rc.arrived(("ou", p, 0))
        rc.start(("fou", p), o_all.at[(3,) + first], o_all.at[(2,) + first], up_t)
        rc.arrived(("od", p, 0))
        rc.arrived(("od", p, 1))
        rc.start(("fod", p), o_all.at[(1,) + last], o_all.at[(2,) + last], dn_t)
        rc.arrived(("ou", p, 1))

    for d in range(1, cp_size):
        rc.arrived(("pos", d))
    sub = lax.broadcasted_iota(jnp.int32, pos_all.shape, 1)
    lane = lax.broadcasted_iota(jnp.int32, pos_all.shape, 2)
    first_tok = (lane == 0) & ((sub == 0) | (sub == piece // BLK))
    far_ref[0] = jnp.max(jnp.where(first_tok, pos_all[...], 0))

    forward_o(0)
    spread_near(3)
    spread_near(1)
    forward_o(1)
    spread_near(2)
    for r in (3, 1, 2):
        spread_far(r)
    loads["wo"].wait()
    for r in (3, 1, 2):
        for i in range(4):
            rc.arrived(("m%d" % i, r))

    for p in range(2):
        rc.arrived(("fou", p))
        rc.arrived(("fod", p))
        at = pl.ds(p * piece, piece)

        def out_tile(i, carry):
            cols = pl.ds(pl.multiple_of(i * TILE, TILE), TILE)
            acc = jnp.dot(o_all[0, at, :], w_all[0, :, cols], preferred_element_type=F32)
            for r in range(1, 4):
                acc += jnp.dot(o_all[r, at, :], w_all[r, :, cols], preferred_element_type=F32)
            x_cols = pl.ds(pl.multiple_of(my_cols + i * TILE, TILE), TILE)
            y_v[at, cols] = (x_v[at, x_cols].astype(F32) + acc).astype(BF16)
            return carry

        lax.fori_loop(0, half // TILE, out_tile, 0)
        lo, hi = pl.ds(p * piece, BLK), pl.ds(p * piece + BLK, BLK)
        cols = pl.ds(my_cols, half)
        rc.start(("yd", p), y_v.at[lo], y_hbm.at[lo, cols], dn_t)
        rc.start(("yu", p), y_v.at[hi], y_hbm.at[hi, cols], up_t)
        load(("y", p), y_v.at[at], y_hbm.at[at, cols])

    for name in ("k_out", "v_out", ("y", 0), ("y", 1)):
        loads[name].wait()
    rc.drain()
    for p in range(2):
        rc.arrived(("yd", p))
        rc.arrived(("yu", p))


def fused_layer(cp_size, tp_size, x_in, pos_in_doc, norm_gain, w_q, w_k, w_v, w_o, inv_freq):
    rows, d_model = x_in.shape
    q_cols, kv_cols = w_q.shape[1], w_k.shape[1]
    head_dim = 2 * inv_freq.shape[0]
    kv_heads = kv_cols // head_dim
    piece, half = rows // 2, d_model // 2
    vm = pltpu.VMEM
    copies = 6 + (cp_size - 1) + 4 + 3 * 9 + 8 + 4 + 4 + 4
    any_spec = pl.BlockSpec(memory_space=pl.ANY)
    return pl.pallas_call(
        functools.partial(layer_kernel, cp_size, tp_size),
        name="fused_layer",
        out_shape=[
            jax.ShapeDtypeStruct((rows, d_model), BF16),
            jax.ShapeDtypeStruct((rows, kv_heads, head_dim), BF16),
            jax.ShapeDtypeStruct((rows, kv_heads, head_dim), BF16),
            jax.ShapeDtypeStruct((1,), jnp.int32),
        ],
        in_specs=[any_spec] * 8,
        out_specs=[any_spec] * 3 + [pl.BlockSpec(memory_space=pltpu.SMEM)],
        scratch_shapes=[
            vm((rows, d_model), BF16), vm((rows, d_model), BF16),
            vm(w_q.shape, BF16), vm(w_k.shape, BF16), vm(w_v.shape, BF16),
            vm((tp_size, q_cols, half), BF16), vm((2, q_cols // cp_size // 2, half), BF16),
            vm((tp_size, rows, q_cols), BF16), vm((rows, half), BF16), vm((rows, q_cols), BF16),
            vm((2, HALO + piece, kv_cols), BF16), vm((2, HALO + piece, kv_cols), BF16),
            vm((rows, kv_heads, head_dim), BF16), vm((rows, kv_heads, head_dim), BF16),
            vm((rows // BLK, BLK), jnp.int32), vm((1, d_model), F32), vm((1, head_dim // 2), F32),
            vm((rows, head_dim), F32), vm((rows, head_dim), F32), vm((rows, BLK), jnp.int32),
            vm((cp_size, rows // BLK, BLK), jnp.int32),
            pltpu.SemaphoreType.DMA((20,)),
            pltpu.SemaphoreType.DMA((copies,)), pltpu.SemaphoreType.DMA((copies,)),
        ],
        compiler_params=pltpu.CompilerParams(collective_id=0, has_side_effects=True, vmem_limit_bytes=60 * 1024 * 1024),
    )(x_in, pos_in_doc.reshape(rows // BLK, BLK), norm_gain.reshape(1, d_model), w_q, w_k, w_v, w_o, inv_freq.reshape(1, head_dim // 2))


def gather_kernel(axis, size, part_hbm, all_hbm, load_sem, send_sems, recv_sems):
    me = lax.axis_index(axis)
    barrier = pltpu.get_barrier_semaphore()
    for d in range(1, size):
        pl.semaphore_signal(barrier, inc=1, device_id={axis: lax.rem(me + d, size)}, device_id_type=MESH)
    pl.semaphore_wait(barrier, size - 1)
    own = pltpu.make_async_copy(part_hbm, all_hbm.at[me], load_sem)
    own.start()
    copies = []
    for d in range(1, size):
        copies.append(pltpu.make_async_remote_copy(src_ref=part_hbm, dst_ref=all_hbm.at[me], send_sem=send_sems.at[d - 1], recv_sem=recv_sems.at[d - 1], device_id={axis: lax.rem(me + d, size)}, device_id_type=MESH))
        copies[-1].start()
    for copy in copies:
        copy.wait()
    own.wait()


def gather(part, axis, size, collective_id):
    any_spec = pl.BlockSpec(memory_space=pl.ANY)
    return pl.pallas_call(
        functools.partial(gather_kernel, axis, size),
        name="gather_%d" % collective_id,
        out_shape=jax.ShapeDtypeStruct((size,) + part.shape, part.dtype),
        in_specs=[any_spec],
        out_specs=any_spec,
        scratch_shapes=[pltpu.SemaphoreType.DMA, pltpu.SemaphoreType.DMA((size - 1,)), pltpu.SemaphoreType.DMA((size - 1,))],
        compiler_params=pltpu.CompilerParams(collective_id=collective_id, has_side_effects=True),
    )(part)


def rope_ref(vectors, cos_t, sin_t):
    half_dim = vectors.shape[-1] // 2
    lower_half = vectors[..., :half_dim].astype(F32)
    upper_half = vectors[..., half_dim:].astype(F32)
    return jnp.concatenate([lower_half * cos_t - upper_half * sin_t, upper_half * cos_t + lower_half * sin_t], axis=-1).astype(BF16)


def global_index(stored_pos, local_rows, cp_size):
    piece_len = local_rows // 2
    owner = stored_pos // local_rows
    within = stored_pos % local_rows
    piece_id = jnp.where(within < piece_len, owner, 2 * cp_size - 1 - owner)
    return piece_id * piece_len + within % piece_len


def general_y(cp_size, tp_size, x_in, pos_in_doc, norm_gain, w_q, w_o, inv_freq, k_rot, v_new):
    rows, kv_heads, head_dim = k_rot.shape
    tokens = rows * cp_size
    x_f32 = x_in.astype(F32)
    inv_rms = lax.rsqrt(jnp.mean(x_f32 * x_f32, axis=-1, keepdims=True) + 1e-5)
    normed = (x_f32 * inv_rms * norm_gain).astype(BF16)
    q_new = jnp.dot(normed, w_q, preferred_element_type=F32).astype(BF16).reshape(rows, kv_heads, -1, head_dim)
    angle = pos_in_doc.astype(F32)[:, None] * inv_freq[None, :]
    q_rot = rope_ref(q_new, jnp.cos(angle)[:, None, None, :], jnp.sin(angle)[:, None, None, :])
    keys = gather(k_rot.reshape(rows, kv_heads * head_dim), "cp", cp_size, 1).reshape(tokens, kv_heads, head_dim)
    vals = gather(v_new.reshape(rows, kv_heads * head_dim), "cp", cp_size, 2).reshape(tokens, kv_heads, head_dim)
    q_idx = global_index(lax.axis_index("cp") * rows + jnp.arange(rows), rows, cp_size)
    key_idx = global_index(jnp.arange(tokens), rows, cp_size)

    def attend(block_args):
        q_blk, idx_blk, pos_blk = block_args
        scores = jnp.einsum("qngd,knd->ngqk", q_blk, keys, preferred_element_type=F32) * head_dim ** -0.5
        visible = (key_idx[None, :] >= (idx_blk - pos_blk)[:, None]) & (key_idx[None, :] <= idx_blk[:, None])
        probs = jax.nn.softmax(jnp.where(visible, scores, NEG), axis=-1).astype(BF16)
        return jnp.einsum("ngqk,knd->qngd", probs, vals, preferred_element_type=F32).astype(BF16)

    blocks = rows // BLK
    o_own = lax.map(attend, (q_rot.reshape(blocks, BLK, kv_heads, -1, head_dim), q_idx.reshape(blocks, BLK), pos_in_doc.reshape(blocks, BLK))).reshape(rows, -1)
    o_parts = gather(o_own, "tp", tp_size, 3)
    w_parts = gather(w_o, "tp", tp_size, 4)
    mixed = jnp.einsum("trc,tcd->rd", o_parts, w_parts, preferred_element_type=F32)
    return (x_f32 + mixed).astype(BF16)


def solution(mesh):
    cp_size, tp_size = mesh.shape["cp"], mesh.shape["tp"]

    def local_step(x_in, doc_id, pos_in_doc, norm_gain, w_q, w_k, w_v, w_o, inv_freq):
        y_out, k_rot, v_new, far = fused_layer(cp_size, tp_size, x_in, pos_in_doc, norm_gain, w_q, w_k, w_v, w_o, inv_freq)

        def redo(state):
            y_new = general_y(cp_size, tp_size, x_in, pos_in_doc, norm_gain, w_q, w_o, inv_freq, k_rot, v_new)
            return jnp.zeros_like(state[0]), y_new

        _, y_out = lax.while_loop(lambda state: state[0] > HALO, redo, (far[0], y_out))
        return y_out, k_rot, v_new

    row_spec = P(("dp", "cp"))
    in_specs = (P(("dp", "cp"), None), row_spec, row_spec, P(), P(None, "tp"), P(None, "tp"), P(None, "tp"), P("tp", None), P())
    out_specs = (P(("dp", "cp"), None), P(("dp", "cp"), "tp", None), P(("dp", "cp"), "tp", None))
    return jax.shard_map(local_step, mesh=mesh, in_specs=in_specs, out_specs=out_specs, check_vma=False)
```

time: 286 us -> 80.9 us (0.28)
  waiting for transfers between devices: 137 us -> 0 us
  matrix products: 91.3 us -> 0 us
  Pallas kernels: 0 us -> 74 us
  blocking collectives: 19.8 us -> 0 us
  other arithmetic: 13.8 us -> 0 us
  between operations: 14 us -> 0.72 us
  local copies, waits for them, and re-layouts: 9.33 us -> 5.23 us
    psum x1 -> x0, waiting for transfers between devices: 120 us -> none  [local_step(): full_sum = lax.psum(part_sum, 'tp')]
    pallas_call x0 -> x1, Pallas kernels: none -> 74 us  [fused_layer(): pl.pallas_call(functools.partial(layer_kernel, cp_size, tp_size), name='f...]
    dot_general x8 -> x0, matrix products: 50.4 us -> none  [the longest x4 30.8 us: attend(): jnp.einsum('ngqk,knd->qngd', attn_probs, val_rows, preferred_element_type...]
    sub x4 -> x0, matrix products: 40.9 us -> none  [attend(): attn_probs = jax.nn.softmax(scores, axis=-1).astype(jnp.bfloat16)]
    all_gather x1 -> x0, blocking collectives: 19.8 us -> none  [local_step(): doc_all = lax.all_gather(doc_id, 'cp', tiled=True)]
    all_gather x2 -> x0, waiting for transfers between devices: 16.7 us -> none  [the longest x1 16.6 us: local_step(): v_all = lax.all_gather(v_new, 'cp', tiled=True)]
    convert_element_type x2 -> x0, other arithmetic: 7.08 us -> none  [the longest x1 6.39 us: local_step(): y_out = (x_in.astype(jnp.float32) + full_sum).astype(jnp.bfloat16)]
  transfers between devices with their start and end apart: 3 -> 0, of which waited for: 2 -> 0; matrix products, arithmetic and copies ran while one was open for 6% -> 0% of each run, Pallas kernels for 0% -> 0%
where the time goes in v1:
time: 80.9 us; the launch traced here: 80.8 us
  Pallas kernels  74 us (91%)
  local copies, waits for them, and re-layouts  5.23 us (6%)
  loops' own time  0.85 us (1%)
    pallas_call x1, Pallas kernels, fused_layer(): pl.pallas_call(functools.partial(layer_kernel, cp_size, tp_size), name='f...  74 us
    unnamed x13, local copies, waits for them, and re-layouts  5.23 us

profile of v1, /device:TPU:97, one launch (start us, length us, event | category | flops | bytes accessed | tf_op | source)
XLA Modules:
  0.0 80.8 jit_solution(18057028115838979648)
XLA Ops:
  0.6 0.0 copy-start
  0.6 0.0 copy-start.7
  0.7 0.0 copy-start.8
  0.7 0.0 copy-start.9
  0.7 74.0 %fused_layer.1 = (bf16[512,3072]{1,0:T(8,128)(2,1)}, bf16[512,2,128]{2,1,0:T(2,128)(2,1)}, bf16[512,2,128]{2,1,0:T(2,128)(2,1)S(1)}, s32[1]{0:T(128)}) custom-call(bf16[512,3072]{1,0:T(8,128)(2,1)} %x_hbm.1, s32[4,128]{1,0:T(4,128)} %bitcast.105, f32[1,3072]{1,0:T(1,128)} %bitcast.109, bf16[3072,768]{1,0:T(8,128)(2,1)} %wq_hbm.1, bf16[3072,256]{1,0:T(8,128)(2,1)} %wk_hbm.1, ...), custom_call_target="tpu_custom_call" | custom-call | tf_op jit(solution)/shard_map/fused_layer/pallas_call | solution.py:311
  74.7 0.0 copy-done
  74.7 0.0 copy-done.7
  74.7 0.0 copy-done.8
  74.7 0.0 copy-done.9
  74.8 0.8 %while.18 = (s32[]{:T(128)}, bf16[512,3072]{1,0:T(8,128)(2,1)}, bf16[512,3072]{1,0:T(8,128)(2,1)S(1)}, f32[3072]{0:T(1024)S(1)}, bf16[3072,768]{1,0:T(8,128)(2,1...) while((s32[]{:T(128)}, bf16[512,3072]{1,0:T(8,128)(2,1)}, ...), condition=%region_6.7_spmd, body=%region_0.6_spmd | while | flops 13729406976 | bytes 124459728 | solution.py:423
  75.6 0.0 copy-start.6
  75.6 3.8 %copy.48 = bf16[512,3072]{1,0:T(8,128)(2,1)} copy(bf16[512,3072]{1,0:T(8,128)(2,1)} %get-tuple-element.332) | data formatting | bytes 6291456
  79.4 0.0 copy-done.6
  79.4 0.7 copy.49
  80.1 0.7 copy.50
Async XLA Ops:
  0.6 74.1 %copy-start = (bf16[512,3072]{1,0:T(8,128)(2,1)S(1)}, bf16[512,3072]{1,0:T(8,128)(2,1)}, u32[]{:S(2)}) copy-start(bf16[512,3072]{1,0:T(8,128)(2,1)} %x_hbm.1) | copy-start | bytes 9437188
  0.6 74.1 %copy-start.7 = (s32[512]{0:T(512)S(1)}, s32[512]{0:T(512)}, u32[]{:S(2)}) copy-start(s32[512]{0:T(512)} %param.14) | copy-start | bytes 6148
  0.7 74.1 %copy-start.8 = (f32[64]{0:T(128)S(1)}, f32[64]{0:T(128)}, u32[]{:S(2)}) copy-start(f32[64]{0:T(128)} %param.20) | copy-start | bytes 772
  0.7 74.1 %copy-start.9 = (f32[3072]{0:T(1024)S(1)}, f32[3072]{0:T(1024)}, u32[]{:S(2)}) copy-start(f32[3072]{0:T(1024)} %param.15) | copy-start | bytes 36868
  75.6 3.8 %copy-start.6 = (bf16[512,2,128]{2,1,0:T(2,128)(2,1)S(1)}, bf16[512,2,128]{2,1,0:T(2,128)(2,1)}, u32[]{:S(2)}) copy-start(bf16[512,2,128]{2,1,0:T(2,128)(2,1)} %get-tuple-element.338) | copy-start | bytes 786436

commit v2 on v1

v2 whole, which is shorter than its diff:
```python
import functools
import math

import jax
import jax.numpy as jnp
from jax import lax
from jax.experimental import pallas as pl
from jax.experimental.pallas import tpu as pltpu
from jax.sharding import PartitionSpec as P

MESH = pl.DeviceIdType.MESH
F32 = jnp.float32
BF16 = jnp.bfloat16
HALO = 128
BLK = 128
GROUPS = 3
NEG = -1e30


class Copies:
    def __init__(self, send_sems, recv_sems, ruler):
        self.send_sems, self.recv_sems, self.ruler = send_sems, recv_sems, ruler
        self.made, self.send_slots, self.recv_slots, self.sent, self.due = {}, {}, {}, {}, {}

    def start(self, name, src, dst, device, send_batch=None, recv_batch=None):
        send_slot = self.send_slots.setdefault(send_batch or name, len(self.send_slots))
        recv_slot = self.recv_slots.setdefault(recv_batch or name, len(self.recv_slots))
        copy = pltpu.make_async_remote_copy(src_ref=src, dst_ref=dst, send_sem=self.send_sems.at[send_slot], recv_sem=self.recv_sems.at[recv_slot], device_id=device, device_id_type=MESH)
        size = math.prod(src.shape)
        if send_batch is None:
            self.made[name] = (copy, True)
        else:
            self.made[name] = (copy, False)
            self.sent[send_batch] = self.sent.get(send_batch, 0) + size
        if recv_batch is not None:
            self.due[recv_batch] = self.due.get(recv_batch, 0) + size
        copy.start()

    def wait_size(self, sem, size):
        slabs, depth, width = self.ruler.shape
        total = size // width
        count = next(n for n in range(1, slabs + 1) if total % (16 * n) == 0 and total // n <= depth)
        ref = self.ruler.at[pl.ds(0, count), pl.ds(0, total // count)]
        pltpu.make_async_copy(ref, ref, sem).wait()

    def arrived(self, name):
        self.made[name][0].wait_recv()

    def batch_arrived(self, batch):
        self.wait_size(self.recv_sems.at[self.recv_slots[batch]], self.due[batch])

    def drain(self):
        for copy, alone in self.made.values():
            if alone:
                copy.wait_send()
        for batch, size in self.sent.items():
            self.wait_size(self.send_sems.at[self.send_slots[batch]], size)


def layer_kernel(cp_size, tp_size, x_hbm, pos_hbm, gain_hbm, wq_hbm, wk_hbm, wv_hbm, wo_hbm, freq_hbm,
                 y_out, k_out, v_out, far_hbm,
                 x_v, h_v, wq_v, wkv_v, w_all, w_share, o_all, q_v, k_win, v_win,
                 pos_v, gain_v, freq_v, cos_v, sin_v, posb_v, pos_all, far_s, load_sems, send_sems, recv_sems):
    rows, d_model = x_v.shape
    piece = rows // 2
    half = d_model // 2
    q_cols = q_v.shape[1]
    head_dim = freq_v.shape[1] * 2
    kv_cols = k_win.shape[2]
    kv_heads = kv_cols // head_dim
    group = q_cols // (kv_heads * head_dim)
    gcols = group * head_dim
    share = q_cols // cp_size
    part = share // 2

    me_c = lax.axis_index("cp")
    me_t = lax.axis_index("tp")
    up_t = {"tp": lax.rem(me_t + 1, tp_size)}
    dn_t = {"tp": lax.rem(me_t + tp_size - 1, tp_size)}
    op_t = {"tp": lax.rem(me_t + tp_size // 2, tp_size)}
    up_x = {"cp": lax.rem(me_c + 2, cp_size)}
    dn_x = {"cp": lax.rem(me_c + cp_size - 2, cp_size)}
    mate = {"cp": me_c + 1 - 2 * lax.rem(me_c, 2)}
    nxt = {"cp": lax.rem(me_c + 1, cp_size)}
    prv = {"cp": lax.rem(me_c + cp_size - 1, cp_size)}
    mine = lax.rem(me_t, 2)
    other = 1 - mine
    my_cols = pl.multiple_of(mine * half, half)
    other_cols = pl.multiple_of(other * half, half)

    row0 = pl.multiple_of(me_c * share, share)
    loads = {}

    def load(name, src, dst):
        copy = pltpu.make_async_copy(src, dst, load_sems.at[len(loads)])
        loads[name] = copy
        copy.start()

    load("pos", pos_hbm, pos_v)
    load("freq", freq_hbm, freq_v)
    load("gain", gain_hbm, gain_v)
    load("share", wo_hbm.at[pl.ds(row0, share)], w_share)
    for c in range(rows // BLK):
        load(("x", c), x_hbm.at[pl.ds(c * BLK, BLK)], x_v.at[pl.ds(c * BLK, BLK)])
    load("wk", wk_hbm, wkv_v.at[:, pl.ds(0, kv_cols)])
    load("wv", wv_hbm, wkv_v.at[:, pl.ds(kv_cols, kv_cols)])
    load("wq", wq_hbm, wq_v)
    load("wo", wo_hbm.at[:, pl.ds(my_cols, half)], w_all.at[0])

    barrier = pltpu.get_barrier_semaphore()
    for d in range(1, cp_size):
        pl.semaphore_signal(barrier, inc=1, device_id={"cp": lax.rem(me_c + d, cp_size)}, device_id_type=MESH)
    for peer in (up_t, dn_t, op_t):
        pl.semaphore_signal(barrier, inc=1, device_id=peer, device_id_type=MESH)

    rc = Copies(send_sems, recv_sems, w_all)
    def share_of(who):
        return pl.ds(pl.multiple_of(who * share, share), share)

    def part_of(who, i):
        return pl.ds(pl.multiple_of(who * share + i * part, part), part)

    gw = half // GROUPS

    def group_of(start, g):
        return pl.ds(pl.multiple_of(start + g * gw, gw), gw)

    def send_shares(g):
        here = pl.ds(g * gw, gw)
        rc.start(("w_up", g), w_share.at[:, group_of(other_cols, g)], w_all.at[3, pl.ds(row0, share), here], up_t, "w")
        rc.start(("w_dn", g), w_share.at[:, group_of(other_cols, g)], w_all.at[1, pl.ds(row0, share), here], dn_t, "w")
        rc.start(("w_op", g), w_share.at[:, group_of(my_cols, g)], w_all.at[2, pl.ds(row0, share), here], op_t, "w")

    def spread_own(r, g):
        rc.arrived((("w_dn", "w_op", "w_up")[r - 1], g))
        at = (r, share_of(me_c), pl.ds(g * gw, gw))
        rc.start(("xu", r, g), w_all.at[at], w_all.at[at], up_x, "w")
        rc.start(("xd", r, g), w_all.at[at], w_all.at[at], dn_x, "w")
        rc.start(("m0", r, g), w_all.at[at], w_all.at[at], mate, "w", ("m", g))

    def spread_near(r, g):
        here = pl.ds(g * gw, gw)
        for name, fwd, to_mate, source, i, onward in (("xu", "fu", "m1", dn_x, 0, up_x), ("xd", "fd", "m2", up_x, 1, dn_x)):
            at = (r, part_of(source["cp"], i), here)
            rc.arrived((name, r, g))
            rc.start((fwd, r, g), w_all.at[at], w_all.at[at], onward, "w")
            at = (r, share_of(source["cp"]), here)
            rc.start((to_mate, r, g), w_all.at[at], w_all.at[at], mate, "w", ("m", g))

    def spread_far(r, g):
        at = (r, share_of(lax.rem(me_c + cp_size // 2, cp_size)), pl.ds(g * gw, gw))
        rc.arrived(("fu", r, g))
        rc.arrived(("fd", r, g))
        rc.start(("m3", r, g), w_all.at[at], w_all.at[at], mate, "w", ("m", g))

    loads["pos"].wait()
    loads["freq"].wait()
    pos_all[0] = pos_v[...]
    freq = jnp.concatenate([freq_v[...], freq_v[...]], axis=1)
    sign = jnp.where(lax.broadcasted_iota(jnp.int32, (1, head_dim), 1) < head_dim // 2, -1.0, 1.0).astype(F32)
    left = lax.broadcasted_iota(jnp.int32, (BLK, head_dim), 1) < head_dim // 2
    for c in range(rows // BLK):
        posb_v[pl.ds(c * BLK, BLK), :] = jnp.transpose(jnp.broadcast_to(pos_v[pl.ds(c, 1), :], (BLK, BLK)))
    for c in range(rows // BLK // 2):
        at, up = pl.ds(c * BLK, BLK), pl.ds(piece + c * BLK, BLK)
        angle = jnp.where(left, posb_v[at, :], posb_v[up, :]).astype(F32) * freq
        for out, both in ((cos_v, jnp.cos(angle)), (sin_v, jnp.sin(angle))):
            turned = pltpu.roll(both, head_dim // 2, 1)
            scale = sign if out is sin_v else 1.0
            out[at, :] = jnp.where(left, both, turned) * scale
            out[up, :] = jnp.where(left, turned, both) * scale

    loads["gain"].wait()
    for c in range(rows // BLK):
        loads[("x", c)].wait()

        def norm(i, carry):
            at = pl.ds(pl.multiple_of(c * BLK + i * 32, 32), 32)
            x_f32 = x_v[at, :].astype(F32)
            inv_rms = lax.rsqrt(jnp.mean(x_f32 * x_f32, axis=-1, keepdims=True) + 1e-5)
            h_v[at, :] = (x_f32 * inv_rms * gain_v[...]).astype(BF16)
            return carry

        lax.fori_loop(0, BLK // 32, norm, 0)
        if c == 1:
            pl.semaphore_wait(barrier, cp_size + 2)
            loads["share"].wait()
            send_shares(0)

    def rope(raw, c):
        at = pl.ds(c * BLK, BLK)
        vec = raw.astype(F32)
        return (vec * cos_v[at, :] + pltpu.roll(vec, head_dim // 2, 1) * sin_v[at, :]).astype(BF16)

    def window_at(c):
        return c * BLK // piece, pl.ds(HALO + c * BLK % piece, BLK)

    loads["wk"].wait()
    loads["wv"].wait()
    kv_new = jnp.dot(h_v[...], wkv_v[...], preferred_element_type=F32).astype(BF16)
    for c in range(rows // BLK):
        p, at = window_at(c)
        new = kv_new[c * BLK:(c + 1) * BLK]
        for n in range(kv_heads):
            k_win[p, at, n * head_dim:(n + 1) * head_dim] = rope(new[:, n * head_dim:(n + 1) * head_dim], c)
        v_win[p, at, :] = new[:, kv_cols:]
    tail = pl.ds(piece, HALO)
    halo = pl.ds(0, HALO)
    rc.start("hk_a", k_win.at[0, tail], k_win.at[0, halo], nxt)
    rc.start("hk_b", k_win.at[1, tail], k_win.at[1, halo], prv)
    rc.start("hv_a", v_win.at[0, tail], v_win.at[0, halo], nxt)
    rc.start("hv_b", v_win.at[1, tail], v_win.at[1, halo], prv)

    send_shares(1)
    for d in range(1, cp_size):
        rc.start(("pos", d), pos_hbm, pos_all.at[cp_size - d], {"cp": lax.rem(me_c + d, cp_size)})

    loads["wq"].wait()

    q_new = jnp.dot(h_v[...], wq_v[...], preferred_element_type=F32).astype(BF16)
    for c in range(rows // BLK):
        for n in range(q_cols // head_dim):
            cols = slice(n * head_dim, (n + 1) * head_dim)
            q_v[pl.ds(c * BLK, BLK), cols] = rope(q_new[c * BLK:(c + 1) * BLK, cols], c)

    send_shares(2)
    for r in (3, 1, 2):
        spread_own(r, 0)
    for name in ("hk_a", "hk_b", "hv_a", "hv_b"):
        rc.arrived(name)

    @pl.when(me_c == cp_size - 1)
    def _():
        k_win[1, 0:HALO, :] = k_win[0, piece:piece + HALO, :]
        v_win[1, 0:HALO, :] = v_win[0, piece:piece + HALO, :]

    def send_o(p, n):
        block = (pl.ds(p * piece, piece), pl.ds(n * gcols, gcols))
        rc.start(("ou", p, n), o_all.at[(0,) + block], o_all.at[(3,) + block], up_t, "oy")
        rc.start(("od", p, n), o_all.at[(0,) + block], o_all.at[(1,) + block], dn_t, "oy")

    score_scale = head_dim ** -0.5
    for p in range(2):
        for n in range(kv_heads):
            cols = slice(n * head_dim, (n + 1) * head_dim)
            for b in range(piece // BLK):
                keys = HALO + (b + 1) * BLK
                at = pl.ds(p * piece + b * BLK, BLK)
                q_blk = jnp.concatenate([q_v[at, (n * group + g) * head_dim:(n * group + g + 1) * head_dim] for g in range(group)], axis=0)
                scores = lax.dot_general(q_blk, k_win[p, 0:keys, cols], (((1,), (1,)), ((), ())), preferred_element_type=F32) * score_scale
                key = lax.broadcasted_iota(jnp.int32, (BLK, keys), 1) - HALO
                row = lax.broadcasted_iota(jnp.int32, (BLK, keys), 0) + b * BLK
                back = jnp.concatenate([posb_v[at, :]] * (keys // BLK), axis=1)
                visible = (key <= row) & (key >= row - back)
                scores = jnp.where(visible[None], scores.reshape(group, BLK, keys), NEG)
                top = jnp.max(scores, axis=-1, keepdims=True)
                weights = jnp.exp(scores - top)
                probs = (weights / jnp.sum(weights, axis=-1, keepdims=True)).astype(BF16).reshape(group * BLK, keys)
                o_blk = jnp.dot(probs, v_win[p, 0:keys, cols], preferred_element_type=F32).astype(BF16)
                for g in range(group):
                    o_all[0, at, (n * group + g) * head_dim:(n * group + g + 1) * head_dim] = o_blk[g * BLK:(g + 1) * BLK]
            send_o(p, n)

    def forward_o(p):
        first = (pl.ds(p * piece, piece), pl.ds(0, gcols))
        last = (pl.ds(p * piece, piece), pl.ds((kv_heads - 1) * gcols, gcols))
        rc.arrived(("ou", p, 0))
        rc.start(("fou", p), o_all.at[(3,) + first], o_all.at[(2,) + first], up_t, "oy")
        rc.arrived(("od", p, 0))
        rc.arrived(("od", p, 1))
        rc.start(("fod", p), o_all.at[(1,) + last], o_all.at[(2,) + last], dn_t, "oy")
        rc.arrived(("ou", p, 1))

    def out_tile(p, g):
        at = pl.ds(p * piece, piece)
        cols = pl.ds(g * gw, gw)
        acc = jnp.dot(o_all[0, at, :], w_all[0, :, cols], preferred_element_type=F32)
        for r in range(1, tp_size):
            acc += jnp.dot(o_all[r, at, :], w_all[r, :, cols], preferred_element_type=F32)
        x_cols = group_of(my_cols, g)
        y_out[at, x_cols] = (x_v[at, x_cols].astype(F32) + acc).astype(BF16)
        lo, hi = pl.ds(p * piece, BLK), pl.ds(p * piece + BLK, BLK)
        rc.start(("yd", p, g), y_out.at[lo, x_cols], y_out.at[lo, x_cols], dn_t, "oy")
        rc.start(("yu", p, g), y_out.at[hi, x_cols], y_out.at[hi, x_cols], up_t, "oy")

    for r in (3, 1, 2):
        spread_own(r, 1)
    for win, out in ((k_win, k_out), (v_win, v_out)):
        for c in range(rows // BLK):
            p, at = window_at(c)
            out[pl.ds(c * BLK, BLK)] = jnp.stack([win[p, at, n * head_dim:(n + 1) * head_dim] for n in range(kv_heads)], axis=1)
    for d in range(1, cp_size):
        rc.arrived(("pos", d))
    sub = lax.broadcasted_iota(jnp.int32, pos_all.shape, 1)
    lane = lax.broadcasted_iota(jnp.int32, pos_all.shape, 2)
    first_tok = (lane == 0) & ((sub == 0) | (sub == piece // BLK))
    far_s[0] = jnp.max(jnp.where(first_tok, pos_all[...], 0))
    load("far", far_s, far_hbm)

    for r in (3, 1, 2):
        spread_near(r, 0)
    for r in (3, 1, 2):
        spread_own(r, 2)
    for r in (3, 1, 2):
        spread_near(r, 1)
    forward_o(0)
    for r in (3, 1, 2):
        spread_far(r, 0)
    for r in (3, 1, 2):
        spread_near(r, 2)
    forward_o(1)
    for r in (3, 1, 2):
        spread_far(r, 1)
    loads["wo"].wait()
    rc.batch_arrived(("m", 0))
    rc.arrived(("fou", 0))
    rc.arrived(("fod", 0))
    out_tile(0, 0)
    rc.batch_arrived(("m", 1))
    out_tile(0, 1)
    for r in (3, 1, 2):
        spread_far(r, 2)
    rc.batch_arrived(("m", 2))
    out_tile(0, 2)
    rc.arrived(("fou", 1))
    rc.arrived(("fod", 1))
    for g in range(GROUPS):
        out_tile(1, g)

    loads["far"].wait()
    rc.drain()
    for p in range(2):
        for g in range(GROUPS):
            rc.arrived(("yd", p, g))
            rc.arrived(("yu", p, g))


def fused_layer(cp_size, tp_size, x_in, pos_in_doc, norm_gain, w_q, w_k, w_v, w_o, inv_freq):
    rows, d_model = x_in.shape
    q_cols, kv_cols = w_q.shape[1], w_k.shape[1]
    head_dim = 2 * inv_freq.shape[0]
    kv_heads = kv_cols // head_dim
    piece, half = rows // 2, d_model // 2
    vm = pltpu.VMEM
    copies = 3 * GROUPS + (cp_size - 1) + 4 + 3 * GROUPS * 4 + GROUPS + 8 + 4 + 4 * GROUPS
    any_spec = pl.BlockSpec(memory_space=pl.ANY)
    return pl.pallas_call(
        functools.partial(layer_kernel, cp_size, tp_size),
        name="fused_layer",
        out_shape=[
            vm((rows, d_model), BF16),
            vm((rows, kv_heads, head_dim), BF16),
            vm((rows, kv_heads, head_dim), BF16),
            jax.ShapeDtypeStruct((1,), jnp.int32),
        ],
        in_specs=[pl.BlockSpec(memory_space=pltpu.HBM)] * 8,
        out_specs=[pl.BlockSpec(memory_space=pltpu.VMEM)] * 3 + [any_spec],
        scratch_shapes=[
            vm((rows, d_model), BF16), vm((rows, d_model), BF16),
            vm(w_q.shape, BF16), vm((d_model, 2 * kv_cols), BF16),
            vm((tp_size, q_cols, half), BF16), vm((q_cols // cp_size, d_model), BF16),
            vm((tp_size, rows, q_cols), BF16), vm((rows, q_cols), BF16),
            vm((2, HALO + piece, kv_cols), BF16), vm((2, HALO + piece, kv_cols), BF16),
            vm((rows // BLK, BLK), jnp.int32), vm((1, d_model), F32), vm((1, head_dim // 2), F32),
            vm((rows, head_dim), F32), vm((rows, head_dim), F32), vm((rows, BLK), jnp.int32),
            vm((cp_size, rows // BLK, BLK), jnp.int32),
            pltpu.SMEM((1,), jnp.int32),
            pltpu.SemaphoreType.DMA((13,)),
            pltpu.SemaphoreType.DMA((2 + 4 + cp_size - 1,)), pltpu.SemaphoreType.DMA((copies,)),
        ],
        compiler_params=pltpu.CompilerParams(collective_id=0, has_side_effects=True, vmem_limit_bytes=59 * 1024 * 1024),
    )(x_in, pos_in_doc.reshape(rows // BLK, BLK), norm_gain.reshape(1, d_model), w_q, w_k, w_v, w_o, inv_freq.reshape(1, head_dim // 2))


def store_kernel(y_v, k_v, v_v, y_hbm, k_hbm, v_hbm, sems):
    copies = [pltpu.make_async_copy(k_v, k_hbm, sems.at[0]), pltpu.make_async_copy(v_v, v_hbm, sems.at[1])]
    for i in range(4):
        at = pl.ds(i * y_v.shape[0] // 4, y_v.shape[0] // 4)
        copies.append(pltpu.make_async_copy(y_v.at[at], y_hbm.at[at], sems.at[2 + i]))
    for copy in copies:
        copy.start()
    for copy in copies:
        copy.wait()


def store_outputs(y_v, k_v, v_v):
    return pl.pallas_call(
        store_kernel,
        name="store_outputs",
        out_shape=[jax.ShapeDtypeStruct(a.shape, a.dtype) for a in (y_v, k_v, v_v)],
        in_specs=[pl.BlockSpec(memory_space=pltpu.VMEM)] * 3,
        out_specs=[pl.BlockSpec(memory_space=pltpu.HBM)] * 3,
        scratch_shapes=[pltpu.SemaphoreType.DMA((6,))],
        compiler_params=pltpu.CompilerParams(vmem_limit_bytes=1024 * 1024),
    )(y_v, k_v, v_v)


def gather_kernel(axis, size, part_hbm, all_hbm, load_sem, send_sems, recv_sems):
    me = lax.axis_index(axis)
    barrier = pltpu.get_barrier_semaphore()
    for d in range(1, size):
        pl.semaphore_signal(barrier, inc=1, device_id={axis: lax.rem(me + d, size)}, device_id_type=MESH)
    pl.semaphore_wait(barrier, size - 1)
    own = pltpu.make_async_copy(part_hbm, all_hbm.at[me], load_sem)
    own.start()
    copies = []
    for d in range(1, size):
        copies.append(pltpu.make_async_remote_copy(src_ref=part_hbm, dst_ref=all_hbm.at[me], send_sem=send_sems.at[d - 1], recv_sem=recv_sems.at[d - 1], device_id={axis: lax.rem(me + d, size)}, device_id_type=MESH))
        copies[-1].start()
    for copy in copies:
        copy.wait()
    own.wait()


def gather(part, axis, size, collective_id):
    any_spec = pl.BlockSpec(memory_space=pl.ANY)
    return pl.pallas_call(
        functools.partial(gather_kernel, axis, size),
        name="gather_%d" % collective_id,
        out_shape=jax.ShapeDtypeStruct((size,) + part.shape, part.dtype),
        in_specs=[any_spec],
        out_specs=any_spec,
        scratch_shapes=[pltpu.SemaphoreType.DMA, pltpu.SemaphoreType.DMA((size - 1,)), pltpu.SemaphoreType.DMA((size - 1,))],
        compiler_params=pltpu.CompilerParams(collective_id=collective_id, has_side_effects=True),
    )(part)


def rope_ref(vectors, cos_t, sin_t):
    half_dim = vectors.shape[-1] // 2
    lower_half = vectors[..., :half_dim].astype(F32)
    upper_half = vectors[..., half_dim:].astype(F32)
    return jnp.concatenate([lower_half * cos_t - upper_half * sin_t, upper_half * cos_t + lower_half * sin_t], axis=-1).astype(BF16)


def global_index(stored_pos, local_rows, cp_size):
    piece_len = local_rows // 2
    owner = stored_pos // local_rows
    within = stored_pos % local_rows
    piece_id = jnp.where(within < piece_len, owner, 2 * cp_size - 1 - owner)
    return piece_id * piece_len + within % piece_len


def general_y(cp_size, tp_size, x_in, pos_in_doc, norm_gain, w_q, w_o, inv_freq, k_rot, v_new):
    rows, kv_heads, head_dim = k_rot.shape
    tokens = rows * cp_size
    x_f32 = x_in.astype(F32)
    inv_rms = lax.rsqrt(jnp.mean(x_f32 * x_f32, axis=-1, keepdims=True) + 1e-5)
    normed = (x_f32 * inv_rms * norm_gain).astype(BF16)
    q_new = jnp.dot(normed, w_q, preferred_element_type=F32).astype(BF16).reshape(rows, kv_heads, -1, head_dim)
    angle = pos_in_doc.astype(F32)[:, None] * inv_freq[None, :]
    q_rot = rope_ref(q_new, jnp.cos(angle)[:, None, None, :], jnp.sin(angle)[:, None, None, :])
    keys = gather(k_rot.reshape(rows, kv_heads * head_dim), "cp", cp_size, 1).reshape(tokens, kv_heads, head_dim)
    vals = gather(v_new.reshape(rows, kv_heads * head_dim), "cp", cp_size, 2).reshape(tokens, kv_heads, head_dim)
    q_idx = global_index(lax.axis_index("cp") * rows + jnp.arange(rows), rows, cp_size)
    key_idx = global_index(jnp.arange(tokens), rows, cp_size)

    def attend(block_args):
        q_blk, idx_blk, pos_blk = block_args
        scores = jnp.einsum("qngd,knd->ngqk", q_blk, keys, preferred_element_type=F32) * head_dim ** -0.5
        visible = (key_idx[None, :] >= (idx_blk - pos_blk)[:, None]) & (key_idx[None, :] <= idx_blk[:, None])
        probs = jax.nn.softmax(jnp.where(visible, scores, NEG), axis=-1).astype(BF16)
        return jnp.einsum("ngqk,knd->qngd", probs, vals, preferred_element_type=F32).astype(BF16)

    blocks = rows // BLK
    o_own = lax.map(attend, (q_rot.reshape(blocks, BLK, kv_heads, -1, head_dim), q_idx.reshape(blocks, BLK), pos_in_doc.reshape(blocks, BLK))).reshape(rows, -1)
    o_parts = gather(o_own, "tp", tp_size, 3)
    w_parts = gather(w_o, "tp", tp_size, 4)
    mixed = jnp.einsum("trc,tcd->rd", o_parts, w_parts, preferred_element_type=F32)
    return (x_f32 + mixed).astype(BF16)


def solution(mesh):
    cp_size, tp_size = mesh.shape["cp"], mesh.shape["tp"]

    def local_step(x_in, doc_id, pos_in_doc, norm_gain, w_q, w_k, w_v, w_o, inv_freq):
        y_out, k_rot, v_new, far = fused_layer(cp_size, tp_size, x_in, pos_in_doc, norm_gain, w_q, w_k, w_v, w_o, inv_freq)
        y_out, k_rot, v_new = store_outputs(y_out, k_rot, v_new)

        def redo(state):
            y_new = general_y(cp_size, tp_size, x_in, pos_in_doc, norm_gain, w_q, w_o, inv_freq, k_rot, v_new)
            return jnp.zeros_like(state[0]), y_new

        _, y_out = lax.while_loop(lambda state: state[0] > HALO, redo, (far[0], y_out))
        return y_out, k_rot, v_new

    row_spec = P(("dp", "cp"))
    in_specs = (P(("dp", "cp"), None), row_spec, row_spec, P(), P(None, "tp"), P(None, "tp"), P(None, "tp"), P("tp", None), P())
    out_specs = (P(("dp", "cp"), None), P(("dp", "cp"), "tp", None), P(("dp", "cp"), "tp", None))
    return jax.shard_map(local_step, mesh=mesh, in_specs=in_specs, out_specs=out_specs, check_vma=False)
```

time: 80.9 us -> 69 us (0.85)
  Pallas kernels: 74 us -> 67.4 us
  local copies, waits for them, and re-layouts: 5.23 us -> 0.02 us
    pallas_call x1, Pallas kernels: 74 us -> 65.5 us  [fused_layer(): pl.pallas_call(functools.partial(layer_kernel, cp_size, tp_size), name='f...]
    unnamed x13 -> x6, local copies, waits for them, and re-layouts: 5.23 us -> 0.02 us
    pallas_call x0 -> x1, Pallas kernels: none -> 1.88 us  [store_outputs(): pl.pallas_call(store_kernel, name='store_outputs', out_shape=[jax.ShapeDt...]
where the time goes in v2:
time: 69 us; the launch traced here: 68.9 us
  Pallas kernels  67.4 us (98%)
  between operations  0.85 us (1%)
    pallas_call x1, Pallas kernels, fused_layer(): pl.pallas_call(functools.partial(layer_kernel, cp_size, tp_size), name='f...  65.5 us
    pallas_call x1, Pallas kernels, store_outputs(): pl.pallas_call(store_kernel, name='store_outputs', out_shape=[jax.ShapeDt...  1.88 us

profile of v2, /device:TPU:97, one launch (start us, length us, event | category | flops | bytes accessed | tf_op | source)
XLA Modules:
  0.0 68.9 jit_solution(10763627536892935821)
XLA Ops:
  0.6 65.5 %fused_layer.1 = (bf16[512,3072]{1,0:T(8,128)(2,1)S(1)}, bf16[512,2,128]{2,1,0:T(2,128)(2,1)S(1)}, bf16[512,2,128]{2,1,0:T(2,128)(2,1)S(1)}, s32[1]{0:T(128)}) custom-call(bf16[512,3072]{1,0:T(8,128)(2,1)} %x_hbm.1, s32[4,128]{1,0:T(4,128)} %bitcast.105, f32[1,3072]{1,0:T(1,128)} %bitcast.109, bf16[3072,768]{1,0:T(8,128)(2,1)} %wq_hbm.1, ...), custom_call_target="tpu_custom_call" | custom-call | tf_op jit(solution)/shard_map/fused_layer/pallas_call | solution.py:347
  66.1 0.0 copy-start.5
  66.1 0.0 copy-start.6
  66.1 0.0 copy-start.7
  66.1 1.9 %store_outputs.1 = (bf16[512,3072]{1,0:T(8,128)(2,1)}, bf16[512,2,128]{2,1,0:T(2,128)(2,1)}, bf16[512,2,128]{2,1,0:T(2,128)(2,1)}) custom-call(bf16[512,3072]{1,0:T(8,128)(2,1)S(1)} %get-tuple-element.106.y_v, bf16[512,2,128]{2,1,0:T(2,128)(2,1)S(1)} %get-tuple-element.107.k_v, bf16[512,2,128]{2,1,0:T(2,128)(2,1)S(1)} %get-tuple-element.108.v_v), custom_call_target="tpu_custom_call" | custom-call | tf_op jit(solution)/shard_map/store_outputs/pallas_call | solution.py:387
  68.0 0.0 copy-done.5
  68.0 0.0 copy-done.6
  68.1 0.0 copy-done.7
  68.1 0.7 %while.18 = (s32[]{:T(128)}, bf16[512,3072]{1,0:T(8,128)(2,1)}, bf16[512,3072]{1,0:T(8,128)(2,1)}, f32[3072]{0:T(1024)S(1)}, bf16[3072,768]{1,0:T(8,128)(2,1)}, ...) while((s32[]{:T(128)}, bf16[512,3072]{1,0:T(8,128)(2,1)}, ...), condition=%region_6.7_spmd, body=%region_0.6_spmd | while | flops 13729406976 | bytes 135994064 | solution.py:483
Async XLA Ops:
  66.1 1.9 %copy-start.5 = (s32[512]{0:T(512)S(1)}, s32[512]{0:T(512)}, u32[]{:S(2)}) copy-start(s32[512]{0:T(512)} %param.14) | copy-start | bytes 6148
  66.1 1.9 %copy-start.6 = (f32[64]{0:T(128)S(1)}, f32[64]{0:T(128)}, u32[]{:S(2)}) copy-start(f32[64]{0:T(128)} %param.20) | copy-start | bytes 772
  66.1 1.9 %copy-start.7 = (f32[3072]{0:T(1024)S(1)}, f32[3072]{0:T(1024)}, u32[]{:S(2)}) copy-start(f32[3072]{0:T(1024)} %param.15) | copy-start | bytes 36868

commit v3 on v2

--- a/solution.py
+++ b/solution.py
@@ -14,12 +14,14 @@
 HALO = 128
 BLK = 128
 GROUPS = 3
+EXTRA = 3
+BATCH = ("w", "w", "w", "e")
 NEG = -1e30
 
 
 class Copies:
-    def __init__(self, send_sems, recv_sems, ruler):
-        self.send_sems, self.recv_sems, self.ruler = send_sems, recv_sems, ruler
+    def __init__(self, send_sems, recv_sems, rulers):
+        self.send_sems, self.recv_sems, self.rulers = send_sems, recv_sems, rulers
         self.made, self.send_slots, self.recv_slots, self.sent, self.due = {}, {}, {}, {}, {}
 
     def start(self, name, src, dst, device, send_batch=None, recv_batch=None):
@@ -37,10 +39,12 @@
         copy.start()
 
     def wait_size(self, sem, size):
-        slabs, depth, width = self.ruler.shape
-        total = size // width
-        count = next(n for n in range(1, slabs + 1) if total % (16 * n) == 0 and total // n <= depth)
-        ref = self.ruler.at[pl.ds(0, count), pl.ds(0, total // count)]
+        fits = []
+        for ruler in self.rulers:
+            slabs, depth, width = ruler.shape
+            fits += [(ruler, n, size // width // n) for n in range(1, slabs + 1) if size % (16 * n * width) == 0 and size // width // n <= depth]
+        ruler, count, deep = fits[0]
+        ref = ruler.at[pl.ds(0, count), pl.ds(0, deep)]
         pltpu.make_async_copy(ref, ref, sem).wait()
 
     def arrived(self, name):
@@ -59,7 +63,7 @@
 
 def layer_kernel(cp_size, tp_size, x_hbm, pos_hbm, gain_hbm, wq_hbm, wk_hbm, wv_hbm, wo_hbm, freq_hbm,
                  y_out, k_out, v_out, far_hbm,
-                 x_v, h_v, wq_v, wkv_v, w_all, w_share, o_all, q_v, k_win, v_win,
+                 x_v, h_v, wq_v, wkv_v, w_all, w_ext, w_share, o_all, q_v, k_win, v_win,
                  pos_v, gain_v, freq_v, cos_v, sin_v, posb_v, pos_all, far_s, load_sems, send_sems, recv_sems):
     rows, d_model = x_v.shape
     piece = rows // 2
@@ -106,6 +110,7 @@
     load("wv", wv_hbm, wkv_v.at[:, pl.ds(kv_cols, kv_cols)])
     load("wq", wq_hbm, wq_v)
     load("wo", wo_hbm.at[:, pl.ds(my_cols, half)], w_all.at[0])
+    load("we", wo_hbm.at[:, pl.ds(other_cols, half // GROUPS)], w_ext.at[0])
 
     barrier = pltpu.get_barrier_semaphore()
     for d in range(1, cp_size):
@@ -113,7 +118,7 @@
     for peer in (up_t, dn_t, op_t):
         pl.semaphore_signal(barrier, inc=1, device_id=peer, device_id_type=MESH)
 
-    rc = Copies(send_sems, recv_sems, w_all)
+    rc = Copies(send_sems, recv_sems, (w_all, w_ext))
     def share_of(who):
         return pl.ds(pl.multiple_of(who * share, share), share)
 
@@ -125,33 +130,49 @@
     def group_of(start, g):
         return pl.ds(pl.multiple_of(start + g * gw, gw), gw)
 
+    def w_ref(g):
+        return (w_ext, pl.ds(0, gw)) if g == EXTRA else (w_all, pl.ds(g * gw, gw))
+
     def send_shares(g):
-        here = pl.ds(g * gw, gw)
-        rc.start(("w_up", g), w_share.at[:, group_of(other_cols, g)], w_all.at[3, pl.ds(row0, share), here], up_t, "w")
-        rc.start(("w_dn", g), w_share.at[:, group_of(other_cols, g)], w_all.at[1, pl.ds(row0, share), here], dn_t, "w")
-        rc.start(("w_op", g), w_share.at[:, group_of(my_cols, g)], w_all.at[2, pl.ds(row0, share), here], op_t, "w")
+        buf, here = w_ref(g)
+        near_cols = group_of(my_cols, 0) if g == EXTRA else group_of(other_cols, g)
+        rc.start(("w_up", g), w_share.at[:, near_cols], buf.at[3, pl.ds(row0, share), here], up_t, BATCH[g])
+        rc.start(("w_dn", g), w_share.at[:, near_cols], buf.at[1, pl.ds(row0, share), here], dn_t, BATCH[g])
+        if g != EXTRA:
+            rc.start(("w_op", g), w_share.at[:, group_of(my_cols, g)], w_all.at[2, pl.ds(row0, share), here], op_t, BATCH[g])
+
+    def relay_extra():
+        lo, hi, here = part_of(me_c, 0), part_of(me_c, 1), pl.ds(0, gw)
+        rc.start("e_up", w_all.at[3, lo, here], w_ext.at[2, lo, here], up_t, BATCH[EXTRA])
+        rc.start("e_dn", w_all.at[1, hi, here], w_ext.at[2, hi, here], dn_t, BATCH[EXTRA])
 
     def spread_own(r, g):
-        rc.arrived((("w_dn", "w_op", "w_up")[r - 1], g))
-        at = (r, share_of(me_c), pl.ds(g * gw, gw))
-        rc.start(("xu", r, g), w_all.at[at], w_all.at[at], up_x, "w")
-        rc.start(("xd", r, g), w_all.at[at], w_all.at[at], dn_x, "w")
-        rc.start(("m0", r, g), w_all.at[at], w_all.at[at], mate, "w", ("m", g))
+        if r == 2 and g == EXTRA:
+            rc.arrived("e_up")
+            rc.arrived("e_dn")
+        else:
+            rc.arrived((("w_dn", "w_op", "w_up")[r - 1], g))
+        buf, here = w_ref(g)
+        at = (r, share_of(me_c), here)
+        rc.start(("xu", r, g), buf.at[at], buf.at[at], up_x, BATCH[g])
+        rc.start(("xd", r, g), buf.at[at], buf.at[at], dn_x, BATCH[g])
+        rc.start(("m0", r, g), buf.at[at], buf.at[at], mate, BATCH[g], ("m", g))
 
     def spread_near(r, g):
-        here = pl.ds(g * gw, gw)
+        buf, here = w_ref(g)
         for name, fwd, to_mate, source, i, onward in (("xu", "fu", "m1", dn_x, 0, up_x), ("xd", "fd", "m2", up_x, 1, dn_x)):
             at = (r, part_of(source["cp"], i), here)
             rc.arrived((name, r, g))
-            rc.start((fwd, r, g), w_all.at[at], w_all.at[at], onward, "w")
+            rc.start((fwd, r, g), buf.at[at], buf.at[at], onward, BATCH[g])
             at = (r, share_of(source["cp"]), here)
-            rc.start((to_mate, r, g), w_all.at[at], w_all.at[at], mate, "w", ("m", g))
+            rc.start((to_mate, r, g), buf.at[at], buf.at[at], mate, BATCH[g], ("m", g))
 
     def spread_far(r, g):
-        at = (r, share_of(lax.rem(me_c + cp_size // 2, cp_size)), pl.ds(g * gw, gw))
+        buf, here = w_ref(g)
+        at = (r, share_of(lax.rem(me_c + cp_size // 2, cp_size)), here)
         rc.arrived(("fu", r, g))
         rc.arrived(("fd", r, g))
-        rc.start(("m3", r, g), w_all.at[at], w_all.at[at], mate, "w", ("m", g))
+        rc.start(("m3", r, g), buf.at[at], buf.at[at], mate, BATCH[g], ("m", g))
 
     loads["pos"].wait()
     loads["freq"].wait()
@@ -185,7 +206,7 @@
         if c == 1:
             pl.semaphore_wait(barrier, cp_size + 2)
             loads["share"].wait()
-            send_shares(0)
+            send_shares(1)
 
     def rope(raw, c):
         at = pl.ds(c * BLK, BLK)
@@ -211,7 +232,7 @@
     rc.start("hv_a", v_win.at[0, tail], v_win.at[0, halo], nxt)
     rc.start("hv_b", v_win.at[1, tail], v_win.at[1, halo], prv)
 
-    send_shares(1)
+    send_shares(2)
     for d in range(1, cp_size):
         rc.start(("pos", d), pos_hbm, pos_all.at[cp_size - d], {"cp": lax.rem(me_c + d, cp_size)})
 
@@ -223,9 +244,9 @@
             cols = slice(n * head_dim, (n + 1) * head_dim)
             q_v[pl.ds(c * BLK, BLK), cols] = rope(q_new[c * BLK:(c + 1) * BLK, cols], c)
 
-    send_shares(2)
+    send_shares(0)
     for r in (3, 1, 2):
-        spread_own(r, 0)
+        spread_own(r, 1)
     for name in ("hk_a", "hk_b", "hv_a", "hv_b"):
         rc.arrived(name)
 
@@ -236,8 +257,8 @@
 
     def send_o(p, n):
         block = (pl.ds(p * piece, piece), pl.ds(n * gcols, gcols))
-        rc.start(("ou", p, n), o_all.at[(0,) + block], o_all.at[(3,) + block], up_t, "oy")
-        rc.start(("od", p, n), o_all.at[(0,) + block], o_all.at[(1,) + block], dn_t, "oy")
+        rc.start(("ou", p, n), o_all.at[(0,) + block], o_all.at[(3,) + block], up_t, "o")
+        rc.start(("od", p, n), o_all.at[(0,) + block], o_all.at[(1,) + block], dn_t, "o")
 
     score_scale = head_dim ** -0.5
     for p in range(2):
@@ -260,31 +281,37 @@
                 for g in range(group):
                     o_all[0, at, (n * group + g) * head_dim:(n * group + g + 1) * head_dim] = o_blk[g * BLK:(g + 1) * BLK]
             send_o(p, n)
+            if (p, n) == (1, 0):
+                send_shares(EXTRA)
 
     def forward_o(p):
         first = (pl.ds(p * piece, piece), pl.ds(0, gcols))
         last = (pl.ds(p * piece, piece), pl.ds((kv_heads - 1) * gcols, gcols))
         rc.arrived(("ou", p, 0))
-        rc.start(("fou", p), o_all.at[(3,) + first], o_all.at[(2,) + first], up_t, "oy")
+        rc.start(("fou", p), o_all.at[(3,) + first], o_all.at[(2,) + first], up_t, "o")
         rc.arrived(("od", p, 0))
         rc.arrived(("od", p, 1))
-        rc.start(("fod", p), o_all.at[(1,) + last], o_all.at[(2,) + last], dn_t, "oy")
+        rc.start(("fod", p), o_all.at[(1,) + last], o_all.at[(2,) + last], dn_t, "o")
         rc.arrived(("ou", p, 1))
 
     def out_tile(p, g):
         at = pl.ds(p * piece, piece)
-        cols = pl.ds(g * gw, gw)
-        acc = jnp.dot(o_all[0, at, :], w_all[0, :, cols], preferred_element_type=F32)
+        buf, cols = w_ref(g)
+        acc = jnp.dot(o_all[0, at, :], buf[0, :, cols], preferred_element_type=F32)
         for r in range(1, tp_size):
-            acc += jnp.dot(o_all[r, at, :], w_all[r, :, cols], preferred_element_type=F32)
-        x_cols = group_of(my_cols, g)
+            acc += jnp.dot(o_all[r, at, :], buf[r, :, cols], preferred_element_type=F32)
+        x_cols = group_of(other_cols, 0) if g == EXTRA else group_of(my_cols, g)
         y_out[at, x_cols] = (x_v[at, x_cols].astype(F32) + acc).astype(BF16)
-        lo, hi = pl.ds(p * piece, BLK), pl.ds(p * piece + BLK, BLK)
-        rc.start(("yd", p, g), y_out.at[lo, x_cols], y_out.at[lo, x_cols], dn_t, "oy")
-        rc.start(("yu", p, g), y_out.at[hi, x_cols], y_out.at[hi, x_cols], up_t, "oy")
-
-    for r in (3, 1, 2):
-        spread_own(r, 1)
+        if g in (1, 2):
+            lo, hi = pl.ds(p * piece, BLK), pl.ds(p * piece + BLK, BLK)
+            rc.start(("yd", p, g), y_out.at[lo, x_cols], y_out.at[lo, x_cols], dn_t, "y", "y")
+            rc.start(("yu", p, g), y_out.at[hi, x_cols], y_out.at[hi, x_cols], up_t, "y", "y")
+
+    def each_slot(step, g):
+        for r in (3, 1, 2):
+            step(r, g)
+
+    each_slot(spread_own, 2)
     for win, out in ((k_win, k_out), (v_win, v_out)):
         for c in range(rows // BLK):
             p, at = window_at(c)
@@ -297,42 +324,41 @@
     far_s[0] = jnp.max(jnp.where(first_tok, pos_all[...], 0))
     load("far", far_s, far_hbm)
 
-    for r in (3, 1, 2):
-        spread_near(r, 0)
-    for r in (3, 1, 2):
-        spread_own(r, 2)
-    for r in (3, 1, 2):
-        spread_near(r, 1)
+    each_slot(spread_near, 1)
+    each_slot(spread_own, 0)
+    relay_extra()
+    each_slot(spread_near, 2)
     forward_o(0)
-    for r in (3, 1, 2):
-        spread_far(r, 0)
-    for r in (3, 1, 2):
-        spread_near(r, 2)
+    each_slot(spread_own, EXTRA)
+    each_slot(spread_far, 1)
+    each_slot(spread_near, 0)
     forward_o(1)
-    for r in (3, 1, 2):
-        spread_far(r, 1)
+    each_slot(spread_far, 2)
     loads["wo"].wait()
-    rc.batch_arrived(("m", 0))
+    loads["we"].wait()
+    rc.batch_arrived(("m", 1))
     rc.arrived(("fou", 0))
     rc.arrived(("fod", 0))
-    out_tile(0, 0)
-    rc.batch_arrived(("m", 1))
     out_tile(0, 1)
-    for r in (3, 1, 2):
-        spread_far(r, 2)
     rc.batch_arrived(("m", 2))
     out_tile(0, 2)
+    each_slot(spread_far, 0)
     rc.arrived(("fou", 1))
     rc.arrived(("fod", 1))
-    for g in range(GROUPS):
-        out_tile(1, g)
+    out_tile(1, 1)
+    out_tile(1, 2)
+    each_slot(spread_near, EXTRA)
+    rc.batch_arrived(("m", 0))
+    out_tile(0, 0)
+    out_tile(1, 0)
+    each_slot(spread_far, EXTRA)
+    rc.batch_arrived(("m", EXTRA))
+    out_tile(0, EXTRA)
+    out_tile(1, EXTRA)
 
     loads["far"].wait()
     rc.drain()
-    for p in range(2):
-        for g in range(GROUPS):
-            rc.arrived(("yd", p, g))
-            rc.arrived(("yu", p, g))
+    rc.batch_arrived("y")
 
 
 def fused_layer(cp_size, tp_size, x_in, pos_in_doc, norm_gain, w_q, w_k, w_v, w_o, inv_freq):
@@ -342,7 +368,7 @@
     kv_heads = kv_cols // head_dim
     piece, half = rows // 2, d_model // 2
     vm = pltpu.VMEM
-    copies = 3 * GROUPS + (cp_size - 1) + 4 + 3 * GROUPS * 4 + GROUPS + 8 + 4 + 4 * GROUPS
+    copies = 3 * GROUPS + 4 + (cp_size - 1) + 4 + 3 * (GROUPS + 1) * 4 + (GROUPS + 1) + 8 + 4 + 1
     any_spec = pl.BlockSpec(memory_space=pl.ANY)
     return pl.pallas_call(
         functools.partial(layer_kernel, cp_size, tp_size),
@@ -358,15 +384,15 @@
         scratch_shapes=[
             vm((rows, d_model), BF16), vm((rows, d_model), BF16),
             vm(w_q.shape, BF16), vm((d_model, 2 * kv_cols), BF16),
-            vm((tp_size, q_cols, half), BF16), vm((q_cols // cp_size, d_model), BF16),
+            vm((tp_size, q_cols, half), BF16), vm((tp_size, q_cols, half // GROUPS), BF16), vm((q_cols // cp_size, d_model), BF16),
             vm((tp_size, rows, q_cols), BF16), vm((rows, q_cols), BF16),
             vm((2, HALO + piece, kv_cols), BF16), vm((2, HALO + piece, kv_cols), BF16),
             vm((rows // BLK, BLK), jnp.int32), vm((1, d_model), F32), vm((1, head_dim // 2), F32),
             vm((rows, head_dim), F32), vm((rows, head_dim), F32), vm((rows, BLK), jnp.int32),
             vm((cp_size, rows // BLK, BLK), jnp.int32),
             pltpu.SMEM((1,), jnp.int32),
-            pltpu.SemaphoreType.DMA((13,)),
-            pltpu.SemaphoreType.DMA((2 + 4 + cp_size - 1,)), pltpu.SemaphoreType.DMA((copies,)),
+            pltpu.SemaphoreType.DMA((14,)),
+            pltpu.SemaphoreType.DMA((4 + 4 + cp_size - 1,)), pltpu.SemaphoreType.DMA((copies,)),
         ],
         compiler_params=pltpu.CompilerParams(collective_id=0, has_side_effects=True, vmem_limit_bytes=59 * 1024 * 1024),
     )(x_in, pos_in_doc.reshape(rows // BLK, BLK), norm_gain.reshape(1, d_model), w_q, w_k, w_v, w_o, inv_freq.reshape(1, head_dim // 2))

time: 69 us -> 66.7 us (0.967)
  Pallas kernels: 67.4 us -> 65 us
    pallas_call x1, Pallas kernels: 65.5 us -> 63.2 us  [fused_layer(): pl.pallas_call(functools.partial(layer_kernel, cp_size, tp_size), name='f...]
where the time goes in v3:
time: 66.7 us; the launch traced here: 66.6 us
  Pallas kernels  65 us (97%)
  between operations  0.85 us (1%)
  loops' own time  0.69 us (1%)
    pallas_call x1, Pallas kernels, fused_layer(): pl.pallas_call(functools.partial(layer_kernel, cp_size, tp_size), name='f...  63.2 us
    pallas_call x1, Pallas kernels, store_outputs(): pl.pallas_call(store_kernel, name='store_outputs', out_shape=[jax.ShapeDt...  1.88 us

profile of v3, /device:TPU:97, one launch (start us, length us, event | category | flops | bytes accessed | tf_op | source)
XLA Modules:
  0.0 66.6 jit_solution(12330264336716177367)
XLA Ops:
  0.6 63.2 %fused_layer.1 = (bf16[512,3072]{1,0:T(8,128)(2,1)S(1)}, bf16[512,2,128]{2,1,0:T(2,128)(2,1)S(1)}, bf16[512,2,128]{2,1,0:T(2,128)(2,1)S(1)}, s32[1]{0:T(128)}) custom-call(bf16[512,3072]{1,0:T(8,128)(2,1)} %x_hbm.1, s32[4,128]{1,0:T(4,128)} %bitcast.105, f32[1,3072]{1,0:T(1,128)} %bitcast.109, bf16[3072,768]{1,0:T(8,128)(2,1)} %wq_hbm.1, ...), custom_call_target="tpu_custom_call" | custom-call | tf_op jit(solution)/shard_map/fused_layer/pallas_call | solution.py:373
  63.8 0.0 copy-start.5
  63.8 0.0 copy-start.6
  63.8 0.0 copy-start.7
  63.8 1.9 %store_outputs.1 = (bf16[512,3072]{1,0:T(8,128)(2,1)}, bf16[512,2,128]{2,1,0:T(2,128)(2,1)}, bf16[512,2,128]{2,1,0:T(2,128)(2,1)}) custom-call(bf16[512,3072]{1,0:T(8,128)(2,1)S(1)} %get-tuple-element.106.y_v, bf16[512,2,128]{2,1,0:T(2,128)(2,1)S(1)} %get-tuple-element.107.k_v, bf16[512,2,128]{2,1,0:T(2,128)(2,1)S(1)} %get-tuple-element.108.v_v), custom_call_target="tpu_custom_call" | custom-call | tf_op jit(solution)/shard_map/store_outputs/pallas_call | solution.py:413
  65.7 0.0 copy-done.5
  65.7 0.0 copy-done.6
  65.7 0.0 copy-done.7
  65.8 0.7 %while.18 = (s32[]{:T(128)}, bf16[512,3072]{1,0:T(8,128)(2,1)}, bf16[512,3072]{1,0:T(8,128)(2,1)}, f32[3072]{0:T(1024)S(1)}, bf16[3072,768]{1,0:T(8,128)(2,1)}, ...) while((s32[]{:T(128)}, bf16[512,3072]{1,0:T(8,128)(2,1)}, ...), condition=%region_6.7_spmd, body=%region_0.6_spmd | while | flops 13729406976 | bytes 135994064 | solution.py:509
Async XLA Ops:
  63.8 1.9 %copy-start.5 = (s32[512]{0:T(512)S(1)}, s32[512]{0:T(512)}, u32[]{:S(2)}) copy-start(s32[512]{0:T(512)} %param.14) | copy-start | bytes 6148
  63.8 1.9 %copy-start.6 = (f32[64]{0:T(128)S(1)}, f32[64]{0:T(128)}, u32[]{:S(2)}) copy-start(f32[64]{0:T(128)} %param.20) | copy-start | bytes 772
  63.8 1.9 %copy-start.7 = (f32[3072]{0:T(1024)S(1)}, f32[3072]{0:T(1024)}, u32[]{:S(2)}) copy-start(f32[3072]{0:T(1024)} %param.15) | copy-start | bytes 36868

commit v4 on v3

--- a/solution.py
+++ b/solution.py
@@ -15,6 +15,7 @@
 BLK = 128
 GROUPS = 3
 EXTRA = 3
+STORES = 16
 BATCH = ("w", "w", "w", "e")
 NEG = -1e30
 
@@ -400,8 +401,8 @@
 
 def store_kernel(y_v, k_v, v_v, y_hbm, k_hbm, v_hbm, sems):
     copies = [pltpu.make_async_copy(k_v, k_hbm, sems.at[0]), pltpu.make_async_copy(v_v, v_hbm, sems.at[1])]
-    for i in range(4):
-        at = pl.ds(i * y_v.shape[0] // 4, y_v.shape[0] // 4)
+    for i in range(STORES):
+        at = pl.ds(i * (y_v.shape[0] // STORES), y_v.shape[0] // STORES)
         copies.append(pltpu.make_async_copy(y_v.at[at], y_hbm.at[at], sems.at[2 + i]))
     for copy in copies:
         copy.start()
@@ -416,7 +417,7 @@
         out_shape=[jax.ShapeDtypeStruct(a.shape, a.dtype) for a in (y_v, k_v, v_v)],
         in_specs=[pl.BlockSpec(memory_space=pltpu.VMEM)] * 3,
         out_specs=[pl.BlockSpec(memory_space=pltpu.HBM)] * 3,
-        scratch_shapes=[pltpu.SemaphoreType.DMA((6,))],
+        scratch_shapes=[pltpu.SemaphoreType.DMA((2 + STORES,))],
         compiler_params=pltpu.CompilerParams(vmem_limit_bytes=1024 * 1024),
     )(y_v, k_v, v_v)
 

time: 66.7 us -> 66.8 us (level)
  no operation moved by 1% of the time
where the time goes in v4:
time: 66.8 us; the launch traced here: 66.7 us
  Pallas kernels  65.1 us (97%)
  between operations  0.85 us (1%)
  loops' own time  0.69 us (1%)
    pallas_call x1, Pallas kernels, fused_layer(): pl.pallas_call(functools.partial(layer_kernel, cp_size, tp_size), name='f...  63.2 us
    pallas_call x1, Pallas kernels, store_outputs(): pl.pallas_call(store_kernel, name='store_outputs', out_shape=[jax.ShapeDt...  1.98 us

profile of v4, /device:TPU:97, one launch (start us, length us, event | category | flops | bytes accessed | tf_op | source)
XLA Modules:
  0.0 66.7 jit_solution(424883802534265795)
XLA Ops:
  0.6 63.2 %fused_layer.1 = (bf16[512,3072]{1,0:T(8,128)(2,1)S(1)}, bf16[512,2,128]{2,1,0:T(2,128)(2,1)S(1)}, bf16[512,2,128]{2,1,0:T(2,128)(2,1)S(1)}, s32[1]{0:T(128)}) custom-call(bf16[512,3072]{1,0:T(8,128)(2,1)} %x_hbm.1, s32[4,128]{1,0:T(4,128)} %bitcast.105, f32[1,3072]{1,0:T(1,128)} %bitcast.109, bf16[3072,768]{1,0:T(8,128)(2,1)} %wq_hbm.1, ...), custom_call_target="tpu_custom_call" | custom-call | tf_op jit(solution)/shard_map/fused_layer/pallas_call | solution.py:374
  63.8 0.0 copy-start.5
  63.8 0.0 copy-start.6
  63.8 0.0 copy-start.7
  63.8 2.0 %store_outputs.1 = (bf16[512,3072]{1,0:T(8,128)(2,1)}, bf16[512,2,128]{2,1,0:T(2,128)(2,1)}, bf16[512,2,128]{2,1,0:T(2,128)(2,1)}) custom-call(bf16[512,3072]{1,0:T(8,128)(2,1)S(1)} %get-tuple-element.106.y_v, bf16[512,2,128]{2,1,0:T(2,128)(2,1)S(1)} %get-tuple-element.107.k_v, bf16[512,2,128]{2,1,0:T(2,128)(2,1)S(1)} %get-tuple-element.108.v_v), custom_call_target="tpu_custom_call" | custom-call | tf_op jit(solution)/shard_map/store_outputs/pallas_call | solution.py:414
  65.8 0.0 copy-done.5
  65.8 0.0 copy-done.6
  65.8 0.0 copy-done.7
  65.8 0.7 %while.18 = (s32[]{:T(128)}, bf16[512,3072]{1,0:T(8,128)(2,1)}, bf16[512,3072]{1,0:T(8,128)(2,1)}, f32[3072]{0:T(1024)S(1)}, bf16[3072,768]{1,0:T(8,128)(2,1)}, ...) while((s32[]{:T(128)}, bf16[512,3072]{1,0:T(8,128)(2,1)}, ...), condition=%region_6.7_spmd, body=%region_0.6_spmd | while | flops 13729406976 | bytes 135994064 | solution.py:510
Async XLA Ops:
  63.8 2.0 %copy-start.5 = (s32[512]{0:T(512)S(1)}, s32[512]{0:T(512)}, u32[]{:S(2)}) copy-start(s32[512]{0:T(512)} %param.14) | copy-start | bytes 6148
  63.8 2.0 %copy-start.6 = (f32[64]{0:T(128)S(1)}, f32[64]{0:T(128)}, u32[]{:S(2)}) copy-start(f32[64]{0:T(128)} %param.20) | copy-start | bytes 772
  63.8 2.0 %copy-start.7 = (f32[3072]{0:T(1024)S(1)}, f32[3072]{0:T(1024)}, u32[]{:S(2)}) copy-start(f32[3072]{0:T(1024)} %param.15) | copy-start | bytes 36868
